TPU v7x, 128 devices: a whole 4x4x4 slice. The times are simulated.
128 devices in a mesh: batch: 1, ctx: 64 (over z, y, x), seq: 2 (over core).
Axes of the slice: x: 4, y: 4, z: 4, core: 2. Of those that a mesh axis runs over, the one named last changes fastest.
Arguments:
- hidden: bfloat16 [16, 5120], P('batch')
- lengths: int32 [16], P('batch')
- latent_cache: bfloat16 [16, 8192, 512], P('batch', ('ctx', 'seq'))
- rope_keys: bfloat16 [16, 8192, 64], P('batch', ('ctx', 'seq'))
- w_uq: bfloat16 [5120, 128, 128], P(None, 'seq')
- w_qr: bfloat16 [5120, 128, 64], P(None, 'seq')
- w_uk: bfloat16 [128, 128, 512], P('seq')
- w_uv: bfloat16 [128, 512, 128], P('seq')
- w_out: bfloat16 [128, 128, 5120], P('seq')
Outputs:
- output: bfloat16 [16, 5120], P('batch')
All inputs are finite; a program needn't handle non-finite values.
Results may differ from a plain program's by a relative error of at most 0.00571221.
Values are sent between devices in bfloat16 or wider.
A program may use at most 1 GiB of HBM per device.

v0:
```python
import jax
import jax.numpy as jnp
from jax import lax
from jax.sharding import PartitionSpec as P

NEG_FILL = -1.0e30


def solution(mesh):
    seq_size = mesh.shape['seq']
    row_spec = P('batch', None)
    cache_spec = P('batch', ('ctx', 'seq'), None)
    proj_spec = P(None, 'seq', None)
    head_spec = P('seq', None, None)

    def local_step(hidden, lengths, latent_cache, rope_keys, w_uq, w_qr, w_uk, w_uv, w_out):
        t_local = latent_cache.shape[1]
        score_scale = (w_uq.shape[2] + w_qr.shape[2]) ** -0.5
        q_nope = jnp.einsum('bd,dhk->bhk', hidden, w_uq, preferred_element_type=jnp.float32).astype(jnp.bfloat16)
        q_rope = jnp.einsum('bd,dhr->bhr', hidden, w_qr, preferred_element_type=jnp.float32).astype(jnp.bfloat16)
        q_lat = jnp.einsum('bhk,hkc->bhc', q_nope, w_uk, preferred_element_type=jnp.float32).astype(jnp.bfloat16)
        lat_all = lax.all_gather(q_lat, 'seq', axis=1, tiled=True)
        rope_all = lax.all_gather(q_rope, 'seq', axis=1, tiled=True)
        scores = jnp.einsum('bhc,btc->bht', lat_all, latent_cache, preferred_element_type=jnp.float32)
        scores = (scores + jnp.einsum('bhr,btr->bht', rope_all, rope_keys, preferred_element_type=jnp.float32)) * score_scale
        shard_index = lax.axis_index('ctx') * seq_size + lax.axis_index('seq')
        positions = shard_index * t_local + jnp.arange(t_local)
        valid = positions[None, None, :] < lengths[:, None, None]
        scores = jnp.where(valid, scores, NEG_FILL)
        local_max = jnp.max(scores, axis=2)
        weights = jnp.where(valid, jnp.exp(scores - local_max[:, :, None]), 0.0)
        local_sum = jnp.sum(weights, axis=2)
        local_acc = jnp.einsum('bht,btc->bhc', weights.astype(jnp.bfloat16), latent_cache, preferred_element_type=jnp.float32)
        global_max = lax.pmax(local_max, ('ctx', 'seq'))
        rescale = jnp.exp(local_max - global_max)
        acc_heads = lax.psum_scatter(local_acc * rescale[:, :, None], 'seq', scatter_dimension=1, tiled=True)
        sum_heads = lax.psum_scatter(local_sum * rescale, 'seq', scatter_dimension=1, tiled=True)
        acc_heads = lax.psum(acc_heads, 'ctx')
        sum_heads = lax.psum(sum_heads, 'ctx')
        lat_out = (acc_heads / sum_heads[:, :, None]).astype(jnp.bfloat16)
        head_vals = jnp.einsum('bhc,hcv->bhv', lat_out, w_uv, preferred_element_type=jnp.float32).astype(jnp.bfloat16)
        mixed_part = jnp.einsum('bhv,hvd->bd', head_vals, w_out, preferred_element_type=jnp.float32)
        mixed = lax.psum(mixed_part, 'seq')
        return (hidden.astype(jnp.float32) + mixed).astype(jnp.bfloat16)

    return jax.shard_map(local_step, mesh=mesh,
                         in_specs=(row_spec, P('batch'), cache_spec, cache_spec, proj_spec, proj_spec, head_spec, head_spec, head_spec),
                         out_specs=row_spec, check_vma=False)
```

profile of v0, /device:TPU:1, one launch (start us, length us, event | category | flops | bytes accessed | tf_op | source)
XLA Modules:
  0.0 448.6 jit_solution(17789725367167016483)
XLA Ops:
  6.5 0.0 copy-start
  6.5 0.0 all-gather.2.cloned.1.call-start
  6.5 71.4 %fusion = bf16[16,64,128]{2,0,1:T(8,128)(2,1)S(1)} fusion(bf16[5120,64,128]{2,1,0:T(8,128)(2,1)} %param.13, bf16[16,5120]{1,0:T(8,128)(2,1)} %param.9), kind=kOutput, calls=%fused_computation | convolution fusion | flops 1342177280 | bytes 84312064 | tf_op jit(solution)/shard_map/bd,dhk->bhk/dot_general | solution.py:19
  78.0 0.0 copy-start.2
  78.0 0.1 copy.31
  78.1 4.6 %fusion.11 = bf16[64,16,512]{2,1,0:T(8,128)(2,1)S(1)} fusion(bf16[64,128,512]{2,1,0:T(8,128)(2,1)} %param.15, bf16[16,64,128]{2,1,0:T(8,128)(2,1)S(1)} %copy.31), kind=kOutput, calls=%fused_computation.19 | convolution fusion | flops 134217728 | bytes 9699328 | tf_op jit(solution)/shard_map/bhk,hkc->bhc/dot_general | solution.py:21
  82.7 1.6 copy.32
  84.3 0.0 all-gather.2.cloned.1.call-update
  84.3 0.0 reduce-scatter.5.cloned.1.call-start
  84.3 0.0 copy-done.2
  84.3 0.0 copy-start.4
  84.4 0.0 copy-start.3
  84.4 20.8 %fusion.16 = bf16[16,64,64]{2,0,1:T(8,128)(2,1)S(1)} fusion(bf16[5120,64,64]{0,2,1:T(8,128)(2,1)} %param.14, bf16[16,5120]{1,0:T(8,128)(2,1)S(1)} %copy-done.2), kind=kOutput, calls=%fused_computation.24 | convolution fusion | flops 671088640 | bytes 42237952 | tf_op jit(solution)/shard_map/bd,dhr->bhr/dot_general | solution.py:20
  105.2 0.1 copy.30
  105.3 3.2 all_gather.7
  108.4 0.0 copy-done.4
  108.4 0.1 broadcast_compare_fusion
  108.5 0.0 copy-done.3
  108.5 0.5 fusion.22
  109.0 0.0 all-gather.2.cloned.1.call-done
  109.0 0.0 copy-done
  109.0 2.4 fusion.21
  111.4 68.0 %pmax.7 = f32[16,128]{1,0:T(8,128)S(1)} all-reduce(f32[16,128]{1,0:T(8,128)S(1)} %get-tuple-element.7), channel_id=1, replica_groups=mesh['batch'=1,'ctx'=64,'seq'=2] {'ctx','seq'}, use_global_device_ids=true, to_apply=%region_1.2 | all-reduce | flops 2048 | bytes 16384 | tf_op jit(solution)/shard_map/pmax | solution.py:34
  179.5 0.2 fusion.8
  179.7 2.7 convolution_multiply_fusion
  182.4 0.0 reduce-scatter.5.cloned.1.call-update
  182.4 0.0 reduce-scatter.7.cloned.1.call-start
  182.5 0.7 copy.16
  183.2 0.0 reduce-scatter.7.cloned.1.call-update
  183.2 0.0 all-reduce.3.cloned.1.call-start
  183.3 10.4 %reduce-scatter.5.cloned.1.call-done = f32[16,64,512]{2,1,0:T(8,128)} async-done(((f32[16,128,512]{2,1,0:T(8,128)}), f32[16,64,512]{2,1,0:T(8,128)}) %reduce-scatter.5.cloned.1.call-update) | async-done | bytes 2097168 | tf_op jit(solution)/shard_map/reduce_scatter | solution.py:36
  193.6 0.0 all-reduce.3.cloned.1.call-update
  193.7 0.0 all-reduce.5.cloned.1.call-start
  193.7 13.8 %reduce-scatter.7.cloned.1.call-done = f32[64,16]{1,0:T(8,128)} async-done(((f32[128,16]{1,0:T(8,128)}), f32[64,16]{1,0:T(8,128)}) %reduce-scatter.7.cloned.1.call-update) | async-done | bytes 4112
  207.5 0.8 copy.17
  208.3 153.6 %psum.22 = f32[16,64]{1,0:T(8,128)S(1)} all-reduce(f32[16,64]{1,0:T(8,128)S(1)} %copy.17), channel_id=1, replica_groups=mesh['batch'=1,'ctx'=64,'seq'=2] {'ctx'}, use_global_device_ids=true, to_apply=%region_6.7 | all-reduce | flops 1024 | bytes 8192 | tf_op jit(solution)/shard_map/psum | solution.py:39
  362.0 0.0 all-reduce.3.cloned.1.call-done
  362.0 1.8 divide_convert_fusion
  363.8 0.0 copy-start.1
  363.8 31.6 %convolution_bitcast_fusion = f32[16,5120]{1,0:T(8,128)} fusion(bf16[64,128,5120]{2,1,0:T(8,128)(2,1)} %param.17, bf16[64,512,128]{2,1,0:T(8,128)(2,1)} %param.16, bf16[16,64,512]{2,1,0:T(8,128)(2,1)S(1)} %divide_convert_fusion), kind=kOutput, calls=%fused_computation.2 | convolution fusion | flops 1476526080 | bytes 93650944 | tf_op jit(solution)/shard_map/bhv,hvd->bd/dot_general | solution.py:42
  395.5 0.0 all-reduce.5.cloned.1.call-update
  395.5 44.9 %all-reduce.5.cloned.1.call-done = f32[16,5120]{1,0:T(8,128)} async-done(((f32[16,5120]{1,0:T(8,128)}), f32[16,5120]{1,0:T(8,128)}) %all-reduce.5.cloned.1.call-update) | async-done | bytes 327696 | tf_op jit(solution)/shard_map/psum | solution.py:43
  440.4 1.7 add_convert_fusion
  442.1 0.0 copy-done.1
  (2 shorter events, 0.0 us)
Async XLA Ops:
  6.5 102.5 %copy-start = (bf16[16,64,512]{2,1,0:T(8,128)(2,1)S(1)}, bf16[16,64,512]{2,1,0:T(8,128)(2,1)}, u32[]{:S(2)}) copy-start(bf16[16,64,512]{2,1,0:T(8,128)(2,1)} %param.11) | copy-start | bytes 3145732
  6.5 102.4 %all-gather.2.cloned.1.call-start = ((), (), s32[]{:S(2)}) async-start(), calls=%async_computation.2 | async-start | bytes 3145728 | tf_op jit(solution)/shard_map/all_gather | solution.py:22
  78.0 6.4 %copy-start.2 = (bf16[16,5120]{1,0:T(8,128)(2,1)S(1)}, bf16[16,5120]{1,0:T(8,128)(2,1)}, u32[]{:S(2)}) copy-start(bf16[16,5120]{1,0:T(8,128)(2,1)} %param.9) | copy-start | bytes 491524
  84.3 109.4 %reduce-scatter.5.cloned.1.call-start = ((), (), s32[]{:S(2)}) async-start(), calls=%async_computation.3 | async-start | bytes 6291456 | tf_op jit(solution)/shard_map/reduce_scatter | solution.py:36
  84.3 24.1 %copy-start.4 = (s32[16]{0:T(128)S(1)}, s32[16]{0:T(128)}, u32[]{:S(2)}) copy-start(s32[16]{0:T(128)} %param.10) | copy-start | bytes 196
  84.4 24.2 %copy-start.3 = (bf16[16,64,64]{2,1,0:T(8,128)(2,1)S(1)}, bf16[16,64,64]{2,1,0:T(8,128)(2,1)}, u32[]{:S(2)}) copy-start(bf16[16,64,64]{2,1,0:T(8,128)(2,1)} %param.12) | copy-start | bytes 393220
  182.4 25.1 %reduce-scatter.7.cloned.1.call-start = ((), (), s32[]{:S(2)}) async-start(), calls=%async_computation.6 | async-start | bytes 98304
  183.2 178.8 %all-reduce.3.cloned.1.call-start = ((), (), s32[]{:S(2)}) async-start(), calls=%async_computation.4 | async-start | bytes 4194304 | tf_op jit(solution)/shard_map/psum | solution.py:38
  193.7 246.7 %all-reduce.5.cloned.1.call-start = ((), (), s32[]{:S(2)}) async-start(), calls=%async_computation.5 | async-start | bytes 655360 | tf_op jit(solution)/shard_map/psum | solution.py:43
  363.8 78.3 %copy-start.1 = (bf16[16,64,512]{2,1,0:T(8,128)(2,1)S(1)}, bf16[16,64,512]{2,1,0:T(8,128)(2,1)}, u32[]{:S(2)}) copy-start(bf16[16,64,512]{2,1,0:T(8,128)(2,1)} %param.11) | copy-start | bytes 3145732
Sparse Core Ops, SparseCore 0:
  84.4 16.9 all-gather.1
  182.5 11.0 reduce-scatter.4
  195.9 11.5 reduce-scatter.6
  212.3 132.8 all-reduce.2
  395.6 44.7 all-reduce.4
where the time goes:
time: 449 us
  blocking collectives  225 us (50%)
  matrix products  134 us (30%)
  waiting for transfers between devices  69.2 us (15%)
  between operations  13.3 us (3%)
    psum x1, blocking collectives, local_step(): sum_heads = lax.psum(sum_heads, 'ctx')  154 us
    dot_general x1, matrix products, local_step(): jnp.einsum('bd,dhk->bhk', hidden, w_uq, preferred_element_type=jnp.float32)  71.4 us
    pmax x1, blocking collectives, local_step(): global_max = lax.pmax(local_max, ('ctx', 'seq'))  68 us
    psum x1, waiting for transfers between devices, local_step(): mixed = lax.psum(mixed_part, 'seq')  44.9 us
    dot_general x1, matrix products, local_step(): jnp.einsum('bhv,hvd->bd', head_vals, w_out, preferred_element_type=jnp.fl...  31.6 us
    dot_general x1, matrix products, local_step(): jnp.einsum('bd,dhr->bhr', hidden, w_qr, preferred_element_type=jnp.float32)  20.8 us
    unnamed x6, waiting for transfers between devices  13.9 us
    reduce_scatter x1, waiting for transfers between devices, local_step(): lax.psum_scatter(local_acc * rescale[:, :, None], 'seq', scatter_dimensio...  10.4 us
  transfers between devices with their start and end apart: 5, of which 3 were waited for; matrix products, arithmetic and copies ran while one was open for 5% of the time, Pallas kernels for 0%

commit v1 on v0

v1 whole, which is shorter than its diff:
```python
import functools

import jax
import jax.numpy as jnp
from jax import lax
from jax.experimental import pallas as pl
from jax.experimental.pallas import tpu as pltpu
from jax.sharding import PartitionSpec as P

NEG_FILL = -1.0e30
F32 = jnp.float32
BF16 = jnp.bfloat16

SHIFTS = ((0, 0, 0), (1, 0, 0), (0, 0, -1), (0, 1, 0), (0, -1, 0), (-1, 0, -1), (0, -1, 1), (0, 1, 1))
STEPS = ((0, 0), (1, 0), (3, 0), (1, 1), (3, 1), (2, 0), (0, 1), (2, 1))

NT = (((1,), (1,)), ((), ()))


def chip_at(x, y, z):
    return z * 16 + y * 4 + x


def chip_of(group, colour):
    z = group // 2
    y = 2 * (group % 2) + colour // 4
    x = (colour % 4 + 8 - y - z) % 4
    return chip_at(x, y, z)


def kernel(scale, hidden, lengths, latent, rope, wuq, wqr, wuk, wuv, wout, out,
           len_s, hid_s, wq_s, wq_f, wr_s, wuk_s, wuv_s, wout_s, lat_s, rope_s,
           lat_b, rope_b, qp, rs1, q_send, q_all, s_buf, p_buf, acc_send, o_buf,
           v_send, v_all, v_f, y_part, y_sib, y_send, y_all, piece, out_b,
           load_sem, own_sem, c_send, c_recv, r_send, r_recv, rs_send, rs_recv,
           qd_send, qd_recv, a_send, a_recv, v_ssem, v_rsem, d_send, d_recv, y_ssem, y_rsem,
           o_send, o_recv):
    ctx = lax.axis_index('ctx')
    core = lax.axis_index('seq')
    z, y, x = ctx // 16, (ctx // 4) % 4, ctx % 4
    colour = (x + y + z) % 4 + 4 * (y % 2)
    group = z * 2 + y // 2
    other = 1 - core
    row = 2 * colour + core
    dspan = hid_s.shape[2]
    cols = pl.ds(pl.multiple_of(colour * dspan, 128), dspan)
    heads = pl.ds(pl.multiple_of(group * 8, 8), 8)

    def dev(chip, c):
        return (0, chip, c)

    def remote(src, dst, ssem, rsem, device):
        return pltpu.make_async_remote_copy(src_ref=src, dst_ref=dst, send_sem=ssem, recv_sem=rsem,
                                            device_id=device, device_id_type=pl.DeviceIdType.MESH)

    loads = [
        pltpu.make_async_copy(wuq.at[pl.ds(pl.multiple_of(colour * dspan, 128), dspan), heads, :], wq_s, load_sem.at[0]),
        pltpu.make_async_copy(wqr.at[heads, :, cols], wr_s, load_sem.at[1]),
        pltpu.make_async_copy(hidden.at[:, :, cols], hid_s, load_sem.at[2]),
        pltpu.make_async_copy(latent, lat_s, load_sem.at[3]),
        pltpu.make_async_copy(rope, rope_s, load_sem.at[4]),
        pltpu.make_async_copy(wuk.at[heads], wuk_s, load_sem.at[5]),
        pltpu.make_async_copy(wuv.at[heads], wuv_s, load_sem.at[6]),
        pltpu.make_async_copy(wout.at[heads, :, cols], wout_s, load_sem.at[7]),
        pltpu.make_async_copy(lengths, len_s, load_sem.at[8]),
    ]
    for load in loads:
        load.start()

    barrier = pltpu.get_barrier_semaphore()

    def greet(chip, c):
        pl.semaphore_signal(barrier, inc=1, device_id=dev(chip, c), device_id_type=pl.DeviceIdType.MESH)

    me_class = core * 8 + group
    me_tile = colour * 2 + core
    for i in range(1, 16):
        peer = (me_class + i) % 16
        greet(chip_of(peer % 8, colour), peer // 8)
        peer = (me_tile + i) % 16
        greet(chip_of(group, peer // 2), peer % 2)
    sources = []
    for dx, dy, dz in SHIFTS:
        sources.append(chip_at((x + 4 - dx) % 4, (y + 4 - dy) % 4, (z + 4 - dz) % 4))
    for t in range(1, 8):
        for c in range(2):
            greet(sources[t], c)

    loads[0].wait()
    chunk = 64

    @pl.loop(0, dspan // chunk)
    def _(i):
        rows = wq_s[pl.ds(i * chunk, chunk)].astype(F32).reshape(chunk * 8, 128)
        wq_f[pl.ds(pl.multiple_of(i * chunk * 8, 8), chunk * 8), :] = rows

    loads[1].wait()
    loads[2].wait()
    hid = hid_s[...].astype(F32).reshape(16, dspan).astype(BF16)
    for h in range(8):
        w_h = wq_f[pl.ds(h, dspan, stride=8), :].astype(BF16)
        qp[0, pl.ds(h, 16, stride=8), :] = jnp.dot(hid, w_h, preferred_element_type=F32)
    part_r = lax.dot_general(hid, wr_s[...].reshape(512, dspan), NT, preferred_element_type=F32)
    for pair in range(4):
        both = part_r[:, pair * 128:(pair + 1) * 128]
        qp[1, pl.ds(2 * pair, 16, stride=8), :] = both
        qp[1, pl.ds(2 * pair + 1, 16, stride=8), :] = pltpu.roll(both, 64, 1)

    pl.semaphore_wait(barrier, 44)

    started = []

    def pair_rows(c):
        return pl.ds(pl.multiple_of(c * 16, 16), 16)

    for i in range(1, 8):
        peer = (colour + i) % 8
        copy = remote(qp.at[:, pair_rows(peer), :], rs1.at[colour], rs_send.at[peer], rs_recv.at[colour],
                      dev(chip_of(group, peer), core))
        copy.start()
        started.append(copy)
    rs1[colour] = qp[:, pair_rows(colour), :]

    loads[3].wait()
    loads[4].wait()
    own_l = pltpu.make_async_copy(lat_s.at[row], lat_b.at[core], own_sem.at[0])
    own_r = pltpu.make_async_copy(rope_s.at[row], rope_b.at[core], own_sem.at[1])

    def cache_send(t, c):
        dx, dy, dz = SHIFTS[t]
        chip = chip_at((x + 4 + dx) % 4, (y + 4 + dy) % 4, (z + 4 + dz) % 4)
        target = (colour + STEPS[t][0]) % 4 + 4 * ((colour // 4 + STEPS[t][1]) % 2)
        src_row = 2 * target + c
        slot = 2 * t + core
        index = 2 * t + c
        a = remote(lat_s.at[src_row], lat_b.at[slot], c_send.at[index], c_recv.at[slot], dev(chip, c))
        b = remote(rope_s.at[src_row], rope_b.at[slot], r_send.at[index], r_recv.at[slot], dev(chip, c))
        a.start()
        b.start()
        started.extend((a, b))

    for t in (5, 6, 7, 1, 2, 3, 4):
        for c in range(2):
            cache_send(t, c)
    cache_send(0, other)
    own_l.start()
    own_r.start()

    def arrive(dst, rsem):
        remote(dst, dst, rsem, rsem, dev(ctx, other)).wait_recv()

    for i in range(1, 8):
        peer = (colour + i) % 8
        arrive(rs1.at[peer], rs_recv.at[peer])
    total = rs1[0]
    for i in range(1, 8):
        total = total + rs1[i]
    q_nope = total[0].astype(BF16)
    q_rope = jnp.where(lax.broadcasted_iota(jnp.int32, (16, 128), 1) < 64, total[1], 0.0)
    loads[5].wait()
    row_head = lax.broadcasted_iota(jnp.int32, (16, 512), 0) % 8
    q_lat = jnp.zeros((16, 512), F32)
    for h in range(8):
        res = jnp.dot(q_nope, wuk_s[h], preferred_element_type=F32)
        q_lat = jnp.where(row_head == h, res, q_lat)
    for r in range(2):
        q_send[r, :, 0:512] = q_lat[r * 8:(r + 1) * 8].astype(BF16)
        q_send[r, :, 512:640] = q_rope[r * 8:(r + 1) * 8].astype(BF16)
    for i in range(1, 16):
        peer = (me_class + i) % 16
        copy = remote(q_send.at[peer // 8], q_all.at[me_class], qd_send.at[peer], qd_recv.at[me_class],
                      dev(chip_of(peer % 8, colour), peer // 8))
        copy.start()
        started.append(copy)
    q_all[me_class] = q_send[core]

    loads[8].wait()
    length = len_s[row]
    for i in range(1, 16):
        peer = (me_class + i) % 16
        arrive(q_all.at[peer], qd_recv.at[peer])
    own_l.wait()
    own_r.wait()
    queries = q_all[...].astype(F32).reshape(128, 640).astype(BF16)
    lane = lax.broadcasted_iota(jnp.int32, (128, 128), 1)
    arrive(lat_b.at[other], c_recv.at[other])
    arrive(rope_b.at[other], r_recv.at[other])
    top = None
    for t in range(8):
        if t:
            for c in range(2):
                arrive(lat_b.at[2 * t + c], c_recv.at[2 * t + c])
                arrive(rope_b.at[2 * t + c], r_recv.at[2 * t + c])
        keys = lat_b[2 * t:2 * t + 2].reshape(128, 512)
        rkeys = rope_b[2 * t:2 * t + 2].reshape(128, 64)
        s = lax.dot_general(queries[:, 0:512], keys, NT, preferred_element_type=F32)
        s = (s + lax.dot_general(queries[:, 512:576], rkeys, NT, preferred_element_type=F32)) * scale
        s = jnp.where(sources[t] * 128 + lane < length, s, NEG_FILL)
        s_buf[:, t * 128:(t + 1) * 128] = s
        m_t = jnp.max(s, axis=1, keepdims=True)
        top = m_t if top is None else jnp.maximum(top, m_t)
    den = jnp.zeros((128, 1), F32)
    for t in range(8):
        valid = sources[t] * 128 + lane < length
        w = jnp.where(valid, jnp.exp(s_buf[:, t * 128:(t + 1) * 128] - top), 0.0)
        den = den + jnp.sum(w, axis=1, keepdims=True)
        p_buf[:, t * 128:(t + 1) * 128] = w.astype(BF16)
    acc = jnp.dot(p_buf[...], lat_b[...].reshape(1024, 512), preferred_element_type=F32)
    acc_send[:, :, 0:512] = acc.reshape(16, 8, 512)
    acc_send[:, :, 512:640] = jnp.where(lane == 0, top, den).reshape(16, 8, 128)

    for i in range(1, 16):
        peer = (me_class + i) % 16
        copy = remote(acc_send.at[peer], o_buf.at[me_class], a_send.at[peer], a_recv.at[me_class],
                      dev(chip_of(peer % 8, colour), peer // 8))
        copy.start()
        started.append(copy)
    o_buf[me_class] = acc_send[me_class]
    for i in range(1, 16):
        peer = (me_class + i) % 16
        arrive(o_buf.at[peer], a_recv.at[peer])
    finished = []
    for r in range(2):
        m_all = [o_buf[r * 8 + g, :, 512:513] for g in range(8)]
        best = functools.reduce(jnp.maximum, m_all)
        num = jnp.zeros((8, 512), F32)
        den_r = jnp.zeros((8, 1), F32)
        for g in range(8):
            factor = jnp.exp(m_all[g] - best)
            num = num + o_buf[r * 8 + g, :, 0:512] * factor
            den_r = den_r + o_buf[r * 8 + g, :, 513:514] * factor
        finished.append(num / den_r)
    o_lat = jnp.concatenate(finished, axis=0).astype(BF16)
    loads[6].wait()
    row_head = lax.broadcasted_iota(jnp.int32, (16, 128), 0) % 8
    vals = jnp.zeros((16, 128), F32)
    for h in range(8):
        res = jnp.dot(o_lat, wuv_s[h], preferred_element_type=F32)
        vals = jnp.where(row_head == h, res, vals)
    v_send[...] = vals.astype(BF16)
    for i in range(1, 8):
        peer = (colour + i) % 8
        copy = remote(v_send, v_all.at[colour], v_ssem.at[peer], v_rsem.at[colour], dev(chip_of(group, peer), core))
        copy.start()
        started.append(copy)
    v_all[colour] = v_send[...]
    for i in range(1, 8):
        peer = (colour + i) % 8
        arrive(v_all.at[peer], v_rsem.at[peer])

    v_f[...] = v_all[...].astype(F32).reshape(128, 128)
    loads[7].wait()
    mixed = jnp.zeros((16, dspan), F32)
    for h in range(8):
        v_h = v_f[pl.ds(h, 16, stride=8), :].astype(BF16)
        mixed = mixed + jnp.dot(v_h, wout_s[h], preferred_element_type=F32)
    y_part[...] = mixed.reshape(2, 8, dspan)
    swap = remote(y_part.at[other], y_sib, d_send, d_recv, dev(ctx, other))
    swap.start()
    swap.wait_recv()
    y_send[...] = y_part[core] + y_sib[...]
    for i in range(1, 8):
        peer = (group + i) % 8
        copy = remote(y_send, y_all.at[group], y_ssem.at[peer], y_rsem.at[group], dev(chip_of(peer, colour), core))
        copy.start()
        started.append(copy)
    y_all[group] = y_send[...]
    for i in range(1, 8):
        peer = (group + i) % 8
        arrive(y_all.at[peer], y_rsem.at[peer])
    y_sum = y_all[0]
    for g in range(1, 8):
        y_sum = y_sum + y_all[g]
    piece[...] = (hid_s[core].astype(F32) + y_sum).astype(BF16)
    for i in range(1, 16):
        peer = (me_tile + i) % 16
        copy = remote(piece, out_b.at[me_tile], o_send.at[peer], o_recv.at[me_tile],
                      dev(chip_of(group, peer // 2), peer % 2))
        copy.start()
        started.append(copy)
    out_b[me_tile] = piece[...]
    for i in range(1, 16):
        peer = (me_tile + i) % 16
        arrive(out_b.at[peer], o_recv.at[peer])
    for slot in range(16):
        out[slot % 2, :, (slot // 2) * dspan:(slot // 2 + 1) * dspan] = out_b[slot]
    swap.wait_send()
    for copy in started:
        copy.wait_send()


def solution(mesh):
    row_spec = P('batch', None)
    cache_spec = P('batch', ('ctx', 'seq'), None)
    proj_spec = P(None, 'seq', None)
    head_spec = P('seq', None, None)

    def local_step(hidden, lengths, latent_cache, rope_keys, w_uq, w_qr, w_uk, w_uv, w_out):
        scale = (w_uq.shape[2] + w_qr.shape[2]) ** -0.5
        width = hidden.shape[1]
        dspan = width // 8
        vmem, dma = pltpu.VMEM, pltpu.SemaphoreType.DMA
        anywhere = pl.BlockSpec(memory_space=pl.ANY)
        scratch = [
            pltpu.SMEM((16,), jnp.int32),
            vmem((2, 8, dspan), BF16),
            vmem((dspan, 8, 128), BF16),
            vmem((dspan * 8, 128), F32),
            vmem((8, 64, dspan), BF16),
            vmem((8, 128, 512), BF16),
            vmem((8, 512, 128), BF16),
            vmem((8, 128, dspan), BF16),
            vmem((16, 64, 512), BF16),
            vmem((16, 64, 64), BF16),
            vmem((16, 64, 512), BF16),
            vmem((16, 64, 64), BF16),
            vmem((2, 128, 128), F32),
            vmem((8, 2, 16, 128), F32),
            vmem((2, 8, 640), BF16),
            vmem((16, 8, 640), BF16),
            vmem((128, 1024), F32),
            vmem((128, 1024), BF16),
            vmem((16, 8, 640), F32),
            vmem((16, 8, 640), F32),
            vmem((16, 128), BF16),
            vmem((8, 16, 128), BF16),
            vmem((128, 128), F32),
            vmem((2, 8, dspan), F32),
            vmem((8, dspan), F32),
            vmem((8, dspan), F32),
            vmem((8, 8, dspan), F32),
            vmem((8, dspan), BF16),
            vmem((16, 8, dspan), BF16),
            dma((9,)), dma((2,)), dma((16,)), dma((16,)), dma((16,)), dma((16,)), dma((8,)), dma((8,)),
            dma((16,)), dma((16,)), dma((16,)), dma((16,)), dma((8,)), dma((8,)), dma, dma, dma((8,)), dma((8,)),
            dma((16,)), dma((16,)),
        ]
        out = pl.pallas_call(
            functools.partial(kernel, scale),
            out_shape=jax.ShapeDtypeStruct((2, 8, width), BF16),
            in_specs=[anywhere] * 9,
            out_specs=pl.BlockSpec(memory_space=pltpu.VMEM),
            scratch_shapes=scratch,
            compiler_params=pltpu.CompilerParams(collective_id=0, has_side_effects=True,
                                                 vmem_limit_bytes=67043328),
            name='mla_decode',
        )(hidden.reshape(2, 8, width), lengths, latent_cache, rope_keys, w_uq,
          jnp.transpose(w_qr, (1, 2, 0)), w_uk, w_uv, w_out)
        return out.reshape(16, width)

    return jax.shard_map(local_step, mesh=mesh,
                         in_specs=(row_spec, P('batch'), cache_spec, cache_spec, proj_spec, proj_spec, head_spec, head_spec, head_spec),
                         out_specs=row_spec, check_vma=False)
```

time: 449 us -> 55.3 us (0.12)
  blocking collectives: 225 us -> 0 us
  matrix products: 134 us -> 0 us
  waiting for transfers between devices: 69.2 us -> 0 us
  Pallas kernels: 0 us -> 53.6 us
  between operations: 13.3 us -> 0.01 us
    psum x1 -> x0, blocking collectives: 154 us -> none  [local_step(): sum_heads = lax.psum(sum_heads, 'ctx')]
    dot_general x7 -> x0, matrix products: 134 us -> none  [the longest x1 71.4 us: local_step(): jnp.einsum('bd,dhk->bhk', hidden, w_uq, preferred_element_type=jnp.float32)]
    pmax x1 -> x0, blocking collectives: 68 us -> none  [local_step(): global_max = lax.pmax(local_max, ('ctx', 'seq'))]
    pallas_call x0 -> x1, Pallas kernels: none -> 53.6 us  [local_step(): pl.pallas_call(functools.partial(kernel, scale), out_shape=jax.ShapeDtype...]
    psum x2 -> x0, waiting for transfers between devices: 44.9 us -> none  [the longest x1 44.9 us: local_step(): mixed = lax.psum(mixed_part, 'seq')]
    unnamed x6 -> x0, waiting for transfers between devices: 13.9 us -> none
    reduce_scatter x1 -> x0, waiting for transfers between devices: 10.4 us -> none  [local_step(): lax.psum_scatter(local_acc * rescale[:, :, None], 'seq', scatter_dimensio...]
  transfers between devices with their start and end apart: 5 -> 0, of which waited for: 3 -> 0; matrix products, arithmetic and copies ran while one was open for 5% -> 0% of each run, Pallas kernels for 0% -> 0%
where the time goes in v1:
time: 55.3 us; the launch traced here: 55.2 us
  Pallas kernels  53.6 us (97%)
  local copies, waits for them, and re-layouts  1.59 us (3%)
    pallas_call x1, Pallas kernels, local_step(): pl.pallas_call(functools.partial(kernel, scale), out_shape=jax.ShapeDtype...  53.6 us
    unnamed x1, local copies, waits for them, and re-layouts  1.59 us

profile of v1, /device:TPU:1, one launch (start us, length us, event | category | flops | bytes accessed | tf_op | source)
XLA Modules:
  0.0 55.2 jit_solution(13674309665609509719)
XLA Ops:
  0.0 53.6 %mla_decode.1 = bf16[2,8,5120]{2,1,0:T(8,128)(2,1)} custom-call(bf16[2,8,5120]{2,1,0:T(8,128)(2,1)} %bitcast.5, s32[16]{0:T(128)} %lengths.1, bf16[16,64,512]{2,1,0:T(8,128)(2,1)} %latent.1, bf16[16,64,64]{2,1,0:T(8,128)(2,1)} %rope.1, bf16[5120,64,128]{2,1,0:T(8,128)(2,1)} %wuq.1, bf16[64,64,5120]{2,1,0:T(8,128)(2,1)} %bitcast.3, ...), custom_call_target="tpu_custom_call" | custom-call | tf_op jit(solution)/shard_map/mla_decode/pallas_call | solution.py:338
  53.6 1.6 %copy.11 = bf16[16,5120]{1,0:T(8,128)(2,1)} copy(bf16[16,5120]{1,0:T(8,128)(2,1)} %bitcast.4) | data formatting | bytes 327680

commit v2 on v1

v2 whole, which is shorter than its diff:
```python
import functools

import jax
import jax.numpy as jnp
from jax import lax
from jax.experimental import pallas as pl
from jax.experimental.pallas import tpu as pltpu
from jax.sharding import PartitionSpec as P

NEG_FILL = -1.0e30
F32 = jnp.float32
BF16 = jnp.bfloat16

SHIFTS = ((0, 0, 0), (1, 0, 0), (0, 0, -1), (0, 1, 0), (0, -1, 0), (-1, 0, -1), (1, -1, 0), (0, 1, 1))
STEPS = ((0, 0), (1, 0), (3, 0), (1, 1), (3, 1), (2, 0), (0, 1), (2, 1))

NT = (((1,), (1,)), ((), ()))


def chip_at(x, y, z):
    return z * 16 + y * 4 + x


def chip_of(group, colour):
    z = group // 2
    y = 2 * (group % 2) + colour // 4
    x = (colour % 4 + 8 - y - z) % 4
    return chip_at(x, y, z)


def kernel(scale, hidden, lengths, latent, rope, wuq, wqr, wuk, wuv, wout, out,
           len_s, hid_s, hid_r, wq_s, wq_f, wr_s, wuk_s, wuv_s, wout_s, lat_s, rope_s, rope_p,
           lat_b, rope_b, qp, rs1, q_send, q_all, s_buf, p_buf, acc_send, o_buf,
           y_part, y_sib, y_send, y_all, piece, out_b,
           load_sem, own_sem, send_sem, recv_sem):
    ctx = lax.axis_index('ctx')
    core = lax.axis_index('seq')
    z, y, x = ctx // 16, (ctx // 4) % 4, ctx % 4
    colour = (x + y + z) % 4 + 4 * (y % 2)
    group = z * 2 + y // 2
    other = 1 - core
    row = 2 * colour + core
    dspan = hid_s.shape[2]
    cols = pl.ds(pl.multiple_of(colour * dspan, 128), dspan)
    heads = pl.ds(pl.multiple_of(group * 8, 8), 8)

    def dev(chip, c):
        return (0, chip, c)

    def remote(src, dst, phase, device):
        return pltpu.make_async_remote_copy(src_ref=src, dst_ref=dst, send_sem=send_sem.at[phase],
                                            recv_sem=recv_sem.at[phase], device_id=device,
                                            device_id_type=pl.DeviceIdType.MESH)

    def arrived(part, phase):
        remote(part, part, phase, dev(ctx, other)).wait_recv()

    def left(part, phase):
        remote(part, part, phase, dev(ctx, other)).wait_send()

    loads = [
        pltpu.make_async_copy(wuq.at[pl.ds(pl.multiple_of(colour * dspan, 128), dspan), heads, :], wq_s, load_sem.at[0]),
        pltpu.make_async_copy(wqr.at[heads, :, cols], wr_s, load_sem.at[1]),
        pltpu.make_async_copy(hidden.at[:, :, cols], hid_s, load_sem.at[2]),
        pltpu.make_async_copy(latent, lat_s, load_sem.at[3]),
        pltpu.make_async_copy(rope, rope_s, load_sem.at[4]),
        pltpu.make_async_copy(wuk.at[heads], wuk_s, load_sem.at[5]),
        pltpu.make_async_copy(wuv.at[heads], wuv_s, load_sem.at[6]),
        pltpu.make_async_copy(wout.at[heads], wout_s, load_sem.at[7]),
        pltpu.make_async_copy(lengths, len_s, load_sem.at[8]),
        pltpu.make_async_copy(hidden.at[row // 8], hid_r, load_sem.at[9]),
    ]
    for i in (0, 1, 2, 4, 3, 5):
        loads[i].start()

    barrier = pltpu.get_barrier_semaphore()

    def greet(chip, c):
        pl.semaphore_signal(barrier, inc=1, device_id=dev(chip, c), device_id_type=pl.DeviceIdType.MESH)

    me_class = core * 8 + group
    me_tile = colour * 2 + core
    for i in range(1, 16):
        peer = (me_class + i) % 16
        greet(chip_of(peer % 8, colour), peer // 8)
        peer = (me_tile + i) % 16
        greet(chip_of(group, peer // 2), peer % 2)
    sources = []
    for dx, dy, dz in SHIFTS:
        sources.append(chip_at((x + 4 - dx) % 4, (y + 4 - dy) % 4, (z + 4 - dz) % 4))
    for t in range(1, 8):
        for c in range(2):
            greet(sources[t], c)

    loads[0].wait()
    chunk = 64

    @pl.loop(0, dspan // chunk)
    def _(i):
        rows = wq_s[pl.ds(i * chunk, chunk)].astype(F32).reshape(chunk * 8, 128)
        wq_f[pl.ds(pl.multiple_of(i * chunk * 8, 8), chunk * 8), :] = rows

    loads[1].wait()
    loads[2].wait()
    hid = hid_s[...].astype(F32).reshape(16, dspan).astype(BF16)
    for h in range(8):
        w_h = wq_f[pl.ds(h, dspan, stride=8), :].astype(BF16)
        qp[0, pl.ds(h, 16, stride=8), :] = jnp.dot(hid, w_h, preferred_element_type=F32)
    part_r = lax.dot_general(hid, wr_s[...].reshape(512, dspan), NT, preferred_element_type=F32)
    for pair in range(4):
        both = part_r[:, pair * 128:(pair + 1) * 128]
        qp[1, pl.ds(2 * pair, 16, stride=8), :] = both
        qp[1, pl.ds(2 * pair + 1, 16, stride=8), :] = pltpu.roll(both, 64, 1)
    loads[4].wait()
    for b in range(16):
        rope_p[b] = jnp.concatenate([rope_s[b, 0:32, :], rope_s[b, 32:64, :]], axis=1)
    loads[3].wait()

    pl.semaphore_wait(barrier, 44)

    def pair_rows(c):
        return pl.ds(pl.multiple_of(c * 16, 16), 16)

    for i in range(1, 8):
        peer = (colour + i) % 8
        remote(qp.at[:, pair_rows(peer), :], rs1.at[colour], 0, dev(chip_of(group, peer), core)).start()

    def cache_send(t, c):
        dx, dy, dz = SHIFTS[t]
        chip = chip_at((x + 4 + dx) % 4, (y + 4 + dy) % 4, (z + 4 + dz) % 4)
        target = (colour + STEPS[t][0]) % 4 + 4 * ((colour // 4 + STEPS[t][1]) % 2)
        src_row = 2 * target + c
        slot = 2 * t + core
        remote(lat_s.at[src_row], lat_b.at[slot], 1, dev(chip, c)).start()
        remote(rope_p.at[src_row], rope_b.at[slot], 2, dev(chip, c)).start()

    for t in (5, 6, 7):
        for c in range(2):
            cache_send(t, c)
    cache_send(0, other)
    own_l = pltpu.make_async_copy(lat_s.at[row], lat_b.at[core], own_sem.at[0])
    own_r = pltpu.make_async_copy(rope_p.at[row], rope_b.at[core], own_sem.at[1])
    own_l.start()
    own_r.start()
    rs1[colour] = qp[:, pair_rows(colour), :]

    for i in (6, 7, 8, 9):
        loads[i].start()
    loads[5].wait()
    arrived(rs1.at[pl.ds(0, 7)], 0)
    total = rs1[0]
    for i in range(1, 8):
        total = total + rs1[i]
    q_nope = total[0].astype(BF16)
    q_rope = jnp.where(lax.broadcasted_iota(jnp.int32, (16, 128), 1) < 64, total[1], 0.0)
    row_head = lax.broadcasted_iota(jnp.int32, (16, 512), 0) % 8
    q_lat = jnp.zeros((16, 512), F32)
    for h in range(8):
        res = jnp.dot(q_nope, wuk_s[h], preferred_element_type=F32)
        q_lat = jnp.where(row_head == h, res, q_lat)
    for r in range(2):
        q_send[r, :, 0:512] = q_lat[r * 8:(r + 1) * 8].astype(BF16)
        q_send[r, :, 512:640] = q_rope[r * 8:(r + 1) * 8].astype(BF16)
    for i in range(1, 16):
        peer = (me_class + i) % 16
        remote(q_send.at[peer // 8], q_all.at[me_class], 3, dev(chip_of(peer % 8, colour), peer // 8)).start()
    for t in range(1, 5):
        for c in range(2):
            cache_send(t, c)
    q_all[me_class] = q_send[core]

    loads[8].wait()
    loads[9].wait()
    length = len_s[row]
    sub = lax.broadcasted_iota(jnp.int32, (8, dspan), 0)
    resid = jnp.zeros((8, dspan), F32)
    for i in range(8):
        block = hid_r[:, i * dspan:(i + 1) * dspan].astype(F32)
        line = jnp.sum(jnp.where(sub == row % 8, block, 0.0), axis=0, keepdims=True)
        resid = jnp.where(sub == i, line, resid)
    loads[6].wait()
    loads[7].wait()

    own_l.wait()
    own_r.wait()
    arrived(q_all.at[pl.ds(0, 15)], 3)
    arrived(lat_b.at[pl.ds(0, 15)], 1)
    arrived(rope_b.at[pl.ds(0, 15)], 2)
    queries = q_all[...].astype(F32).reshape(128, 640).astype(BF16)
    lane = lax.broadcasted_iota(jnp.int32, (128, 128), 1)
    top = None
    for t in range(8):
        keys = lat_b[2 * t:2 * t + 2].reshape(128, 512)
        packed = rope_b[2 * t:2 * t + 2]
        rkeys = jnp.concatenate([packed[:, :, 0:64], packed[:, :, 64:128]], axis=1).reshape(128, 64)
        s = lax.dot_general(queries[:, 0:512], keys, NT, preferred_element_type=F32)
        s = (s + lax.dot_general(queries[:, 512:576], rkeys, NT, preferred_element_type=F32)) * scale
        s = jnp.where(sources[t] * 128 + lane < length, s, NEG_FILL)
        s_buf[:, t * 128:(t + 1) * 128] = s
        m_t = jnp.max(s, axis=1, keepdims=True)
        top = m_t if top is None else jnp.maximum(top, m_t)
    den = jnp.zeros((128, 1), F32)
    for t in range(8):
        valid = sources[t] * 128 + lane < length
        w = jnp.where(valid, jnp.exp(s_buf[:, t * 128:(t + 1) * 128] - top), 0.0)
        den = den + jnp.sum(w, axis=1, keepdims=True)
        p_buf[:, t * 128:(t + 1) * 128] = w.astype(BF16)
    acc = jnp.dot(p_buf[...], lat_b[...].reshape(1024, 512), preferred_element_type=F32)
    acc_send[:, :, 0:512] = acc.reshape(16, 8, 512)
    acc_send[:, :, 512:640] = jnp.where(lane == 0, top, den).reshape(16, 8, 128)

    for i in range(1, 16):
        peer = (me_class + i) % 16
        remote(acc_send.at[peer], o_buf.at[me_class], 4, dev(chip_of(peer % 8, colour), peer // 8)).start()
    o_buf[me_class] = acc_send[me_class]
    arrived(o_buf.at[pl.ds(0, 15)], 4)
    finished = []
    for r in range(2):
        m_all = [o_buf[r * 8 + g, :, 512:513] for g in range(8)]
        best = functools.reduce(jnp.maximum, m_all)
        num = jnp.zeros((8, 512), F32)
        den_r = jnp.zeros((8, 1), F32)
        for g in range(8):
            factor = jnp.exp(m_all[g] - best)
            num = num + o_buf[r * 8 + g, :, 0:512] * factor
            den_r = den_r + o_buf[r * 8 + g, :, 513:514] * factor
        finished.append(num / den_r)
    o_lat = jnp.concatenate(finished, axis=0).astype(BF16)
    row_head = lax.broadcasted_iota(jnp.int32, (16, 128), 0) % 8
    vals = jnp.zeros((16, 128), F32)
    for h in range(8):
        res = jnp.dot(o_lat, wuv_s[h], preferred_element_type=F32)
        vals = jnp.where(row_head == h, res, vals)

    spread = jnp.concatenate([jnp.where(row_head == h, vals, 0.0) for h in range(8)], axis=1).astype(BF16)
    parts = [jnp.zeros((8, dspan), F32), jnp.zeros((8, dspan), F32)]
    for i in range(8):
        cut = wout_s[:, :, i * dspan:(i + 1) * dspan].reshape(1024, dspan)
        mixed = jnp.dot(spread, cut, preferred_element_type=F32)
        for r in range(2):
            line = jnp.sum(mixed[r * 8:(r + 1) * 8], axis=0, keepdims=True)
            parts[r] = jnp.where(sub == i, line, parts[r])
    y_part[0] = parts[0]
    y_part[1] = parts[1]
    remote(y_part.at[other], y_sib, 5, dev(ctx, other)).start()
    arrived(y_sib, 5)
    y_send[...] = y_part[core] + y_sib[...]
    for i in range(1, 8):
        peer = (group + i) % 8
        remote(y_send, y_all.at[group], 6, dev(chip_of(peer, colour), core)).start()
    y_all[group] = y_send[...]
    arrived(y_all.at[pl.ds(0, 7)], 6)
    y_sum = y_all[0]
    for g in range(1, 8):
        y_sum = y_sum + y_all[g]
    piece[...] = (resid + y_sum).astype(BF16)
    for i in range(1, 16):
        peer = (me_tile + i) % 16
        remote(piece, out_b.at[me_tile], 7, dev(chip_of(group, peer // 2), peer % 2)).start()
    out_b[me_tile] = piece[...]
    arrived(out_b.at[pl.ds(0, 15)], 7)
    out[...] = out_b[...]
    left(rs1.at[pl.ds(0, 7)], 0)
    left(lat_b.at[pl.ds(0, 15)], 1)
    left(rope_b.at[pl.ds(0, 15)], 2)
    left(q_all.at[pl.ds(0, 15)], 3)
    left(o_buf.at[pl.ds(0, 15)], 4)
    left(y_sib, 5)
    left(y_all.at[pl.ds(0, 7)], 6)
    left(out_b.at[pl.ds(0, 15)], 7)


def solution(mesh):
    row_spec = P('batch', None)
    cache_spec = P('batch', ('ctx', 'seq'), None)
    proj_spec = P(None, 'seq', None)
    head_spec = P('seq', None, None)

    def local_step(hidden, lengths, latent_cache, rope_keys, w_uq, w_qr, w_uk, w_uv, w_out):
        scale = (w_uq.shape[2] + w_qr.shape[2]) ** -0.5
        width = hidden.shape[1]
        dspan = width // 8
        vmem, dma = pltpu.VMEM, pltpu.SemaphoreType.DMA
        anywhere = pl.BlockSpec(memory_space=pl.ANY)
        scratch = [
            pltpu.SMEM((16,), jnp.int32),
            vmem((2, 8, dspan), BF16),
            vmem((8, width), BF16),
            vmem((dspan, 8, 128), BF16),
            vmem((dspan * 8, 128), F32),
            vmem((8, 64, dspan), BF16),
            vmem((8, 128, 512), BF16),
            vmem((8, 512, 128), BF16),
            vmem((8, 128, width), BF16),
            vmem((16, 64, 512), BF16),
            vmem((16, 64, 64), BF16),
            vmem((16, 32, 128), BF16),
            vmem((16, 64, 512), BF16),
            vmem((16, 32, 128), BF16),
            vmem((2, 128, 128), F32),
            vmem((8, 2, 16, 128), F32),
            vmem((2, 8, 640), BF16),
            vmem((16, 8, 640), BF16),
            vmem((128, 1024), F32),
            vmem((128, 1024), BF16),
            vmem((16, 8, 640), F32),
            vmem((16, 8, 640), F32),
            vmem((2, 8, dspan), F32),
            vmem((8, dspan), F32),
            vmem((8, dspan), F32),
            vmem((8, 8, dspan), F32),
            vmem((8, dspan), BF16),
            vmem((16, 8, dspan), BF16),
            dma((10,)), dma((2,)), dma((8,)), dma((8,)),
        ]
        out = pl.pallas_call(
            functools.partial(kernel, scale),
            out_shape=jax.ShapeDtypeStruct((16, 8, dspan), BF16),
            in_specs=[anywhere] * 9,
            out_specs=pl.BlockSpec(memory_space=pltpu.VMEM),
            scratch_shapes=scratch,
            compiler_params=pltpu.CompilerParams(collective_id=0, has_side_effects=True,
                                                 vmem_limit_bytes=67043328),
            name='mla_decode',
        )(hidden.reshape(2, 8, width), lengths, latent_cache, rope_keys, w_uq,
          jnp.transpose(w_qr, (1, 2, 0)), w_uk, w_uv, w_out)
        return out.reshape(16, width)

    return jax.shard_map(local_step, mesh=mesh,
                         in_specs=(row_spec, P('batch'), cache_spec, cache_spec, proj_spec, proj_spec, head_spec, head_spec, head_spec),
                         out_specs=row_spec, check_vma=False)
```

time: 55.3 us -> 46.2 us (0.84)
  Pallas kernels: 53.6 us -> 44.4 us
    pallas_call x1, Pallas kernels: 53.6 us -> 44.4 us  [local_step(): pl.pallas_call(functools.partial(kernel, scale), out_shape=jax.ShapeDtype...]
where the time goes in v2:
time: 46.2 us; the launch traced here: 46.1 us
  Pallas kernels  44.4 us (96%)
  local copies, waits for them, and re-layouts  1.6 us (3%)
    pallas_call x1, Pallas kernels, local_step(): pl.pallas_call(functools.partial(kernel, scale), out_shape=jax.ShapeDtype...  44.4 us
    unnamed x1, local copies, waits for them, and re-layouts  1.6 us

profile of v2, /device:TPU:1, one launch (start us, length us, event | category | flops | bytes accessed | tf_op | source)
XLA Modules:
  0.0 46.1 jit_solution(2513333583997941252)
XLA Ops:
  0.0 44.4 %mla_decode.1 = bf16[16,8,640]{2,1,0:T(8,128)(2,1)} custom-call(bf16[2,8,5120]{2,1,0:T(8,128)(2,1)} %bitcast.6, s32[16]{0:T(128)} %lengths.1, bf16[16,64,512]{2,1,0:T(8,128)(2,1)} %latent.1, bf16[16,64,64]{2,1,0:T(8,128)(2,1)} %rope.1, bf16[5120,64,128]{2,1,0:T(8,128)(2,1)} %wuq.1, bf16[64,64,5120]{2,1,0:T(8,128)(2,1)} %bitcast.4, ...), custom_call_target="tpu_custom_call" | custom-call | tf_op jit(solution)/shard_map/mla_decode/pallas_call | solution.py:316
  44.5 1.6 %copy.10 = bf16[2,8,8,640]{3,1,2,0:T(8,128)(2,1)} copy(bf16[2,8,8,640]{3,2,1,0:T(8,128)(2,1)} %bitcast.5) | data formatting | bytes 327680

commit v3 on v2

--- a/solution.py
+++ b/solution.py
@@ -17,25 +17,27 @@
 NT = (((1,), (1,)), ((), ()))
 
 
-def chip_at(x, y, z):
-    return z * 16 + y * 4 + x
-
-
-def chip_of(group, colour):
-    z = group // 2
-    y = 2 * (group % 2) + colour // 4
-    x = (colour % 4 + 8 - y - z) % 4
-    return chip_at(x, y, z)
+CLASS = ((2, 2, 0), (0, 2, 2), (2, 0, 2), (1, 2, 1), (3, 2, 3), (1, 0, 3), (3, 0, 1))
 
 
 def kernel(scale, hidden, lengths, latent, rope, wuq, wqr, wuk, wuv, wout, out,
            len_s, hid_s, hid_r, wq_s, wq_f, wr_s, wuk_s, wuv_s, wout_s, lat_s, rope_s, rope_p,
-           lat_b, rope_b, qp, rs1, q_send, q_all, s_buf, p_buf, acc_send, o_buf,
-           y_part, y_sib, y_send, y_all, piece, out_b,
+           lat_b, rope_b, qp, rs1, q_send, q_all, s_buf, p_buf, acc_send, o_buf, ml_send, ml_all, ml_t,
+           part_a, part_b, sib_a, sib_b, ysend_a, ysend_b, yall_a, yall_b, piece_a, piece_b, out_a, out_b,
            load_sem, own_sem, send_sem, recv_sem):
     ctx = lax.axis_index('ctx')
     core = lax.axis_index('seq')
     z, y, x = ctx // 16, (ctx // 4) % 4, ctx % 4
+    xs = [(x + d) % 4 for d in range(4)]
+    ys = [(y + d) % 4 for d in range(4)]
+    zs = [(z + d) % 4 for d in range(4)]
+    ys4 = [v * 4 for v in ys]
+    zs16 = [v * 16 for v in zs]
+
+    def chip_at(offset, sign=1):
+        dx, dy, dz = offset
+        return zs16[sign * dz % 4] + ys4[sign * dy % 4] + xs[sign * dx % 4]
+
     colour = (x + y + z) % 4 + 4 * (y % 2)
     group = z * 2 + y // 2
     other = 1 - core
@@ -80,15 +82,23 @@
 
     me_class = core * 8 + group
     me_tile = colour * 2 + core
-    for i in range(1, 16):
-        peer = (me_class + i) % 16
-        greet(chip_of(peer % 8, colour), peer // 8)
-        peer = (me_tile + i) % 16
-        greet(chip_of(group, peer // 2), peer % 2)
-    sources = []
-    for dx, dy, dz in SHIFTS:
-        sources.append(chip_at((x + 4 - dx) % 4, (y + 4 - dy) % 4, (z + 4 - dz) % 4))
-    for t in range(1, 8):
+    class_chips = [(chip_at(o), zs[o[2]] * 2 + ys[o[1]] // 2) for o in CLASS]
+    class_peers = [(chip, c, c * 8 + g) for chip, g in class_chips for c in range(2)] + [(ctx, other, other * 8 + group)]
+    mate = y + 1 - 2 * (y % 2)
+    tile_chips = []
+    for d in (2, 1, 3):
+        tile_chips.append((z * 16 + mate * 4 + xs[d], (xs[d] + mate + z) % 4 + 4 * (mate % 2)))
+    tile_chips.append((zs16[0] + ys4[0] + xs[2], (xs[2] + y + z) % 4 + 4 * (y % 2)))
+    tile_chips.append((z * 16 + mate * 4 + x, (x + mate + z) % 4 + 4 * (mate % 2)))
+    for d in (1, 3):
+        tile_chips.append((zs16[0] + ys4[0] + xs[d], (xs[d] + y + z) % 4 + 4 * (y % 2)))
+    tile_peers = [(chip, c, j) for chip, j in tile_chips for c in range(2)] + [(ctx, other, colour)]
+    for chip, c, _ in class_peers[:-1]:
+        greet(chip, c)
+    for chip, c, _ in tile_peers:
+        greet(chip, c)
+    sources = [chip_at(o, -1) for o in SHIFTS]
+    for t in (5, 6, 7, 1, 2, 3, 4):
         for c in range(2):
             greet(sources[t], c)
 
@@ -116,18 +126,16 @@
         rope_p[b] = jnp.concatenate([rope_s[b, 0:32, :], rope_s[b, 32:64, :]], axis=1)
     loads[3].wait()
 
-    pl.semaphore_wait(barrier, 44)
+    pl.semaphore_wait(barrier, 43)
 
     def pair_rows(c):
         return pl.ds(pl.multiple_of(c * 16, 16), 16)
 
-    for i in range(1, 8):
-        peer = (colour + i) % 8
-        remote(qp.at[:, pair_rows(peer), :], rs1.at[colour], 0, dev(chip_of(group, peer), core)).start()
+    for chip, peer in tile_chips:
+        remote(qp.at[:, pair_rows(peer), :], rs1.at[colour], 0, dev(chip, core)).start()
 
     def cache_send(t, c):
-        dx, dy, dz = SHIFTS[t]
-        chip = chip_at((x + 4 + dx) % 4, (y + 4 + dy) % 4, (z + 4 + dz) % 4)
+        chip = chip_at(SHIFTS[t])
         target = (colour + STEPS[t][0]) % 4 + 4 * ((colour // 4 + STEPS[t][1]) % 2)
         src_row = 2 * target + c
         slot = 2 * t + core
@@ -161,9 +169,8 @@
     for r in range(2):
         q_send[r, :, 0:512] = q_lat[r * 8:(r + 1) * 8].astype(BF16)
         q_send[r, :, 512:640] = q_rope[r * 8:(r + 1) * 8].astype(BF16)
-    for i in range(1, 16):
-        peer = (me_class + i) % 16
-        remote(q_send.at[peer // 8], q_all.at[me_class], 3, dev(chip_of(peer % 8, colour), peer // 8)).start()
+    for chip, c, _ in class_peers:
+        remote(q_send.at[c], q_all.at[me_class], 3, dev(chip, c)).start()
     for t in range(1, 5):
         for c in range(2):
             cache_send(t, c)
@@ -206,24 +213,29 @@
         den = den + jnp.sum(w, axis=1, keepdims=True)
         p_buf[:, t * 128:(t + 1) * 128] = w.astype(BF16)
     acc = jnp.dot(p_buf[...], lat_b[...].reshape(1024, 512), preferred_element_type=F32)
-    acc_send[:, :, 0:512] = acc.reshape(16, 8, 512)
-    acc_send[:, :, 512:640] = jnp.where(lane == 0, top, den).reshape(16, 8, 128)
-
-    for i in range(1, 16):
-        peer = (me_class + i) % 16
-        remote(acc_send.at[peer], o_buf.at[me_class], 4, dev(chip_of(peer % 8, colour), peer // 8)).start()
+    acc_send[...] = acc.reshape(16, 8, 512)
+    ml_send[...] = jnp.where(lane == 0, top, den).T[0:2]
+
+    for chip, c, _ in class_peers:
+        remote(ml_send, ml_all.at[me_class], 5, dev(chip, c)).start()
+    for chip, c, peer in class_peers:
+        remote(acc_send.at[peer], o_buf.at[me_class], 4, dev(chip, c)).start()
     o_buf[me_class] = acc_send[me_class]
+    ml_all[me_class] = ml_send[...]
+    arrived(ml_all.at[pl.ds(0, 15)], 5)
+    ml_t[:, 0:32] = ml_all[...].reshape(32, 128).T
+    ml = ml_t[pl.ds(pl.multiple_of(me_class * 8, 8), 8), :]
     arrived(o_buf.at[pl.ds(0, 15)], 4)
     finished = []
     for r in range(2):
-        m_all = [o_buf[r * 8 + g, :, 512:513] for g in range(8)]
+        m_all = [ml[:, 2 * (r * 8 + g):2 * (r * 8 + g) + 1] for g in range(8)]
         best = functools.reduce(jnp.maximum, m_all)
         num = jnp.zeros((8, 512), F32)
         den_r = jnp.zeros((8, 1), F32)
         for g in range(8):
             factor = jnp.exp(m_all[g] - best)
-            num = num + o_buf[r * 8 + g, :, 0:512] * factor
-            den_r = den_r + o_buf[r * 8 + g, :, 513:514] * factor
+            num = num + o_buf[r * 8 + g] * factor
+            den_r = den_r + ml[:, 2 * (r * 8 + g) + 1:2 * (r * 8 + g) + 2] * factor
         finished.append(num / den_r)
     o_lat = jnp.concatenate(finished, axis=0).astype(BF16)
     row_head = lax.broadcasted_iota(jnp.int32, (16, 128), 0) % 8
@@ -233,41 +245,63 @@
         vals = jnp.where(row_head == h, res, vals)
 
     spread = jnp.concatenate([jnp.where(row_head == h, vals, 0.0) for h in range(8)], axis=1).astype(BF16)
-    parts = [jnp.zeros((8, dspan), F32), jnp.zeros((8, dspan), F32)]
-    for i in range(8):
-        cut = wout_s[:, :, i * dspan:(i + 1) * dspan].reshape(1024, dspan)
-        mixed = jnp.dot(spread, cut, preferred_element_type=F32)
-        for r in range(2):
-            line = jnp.sum(mixed[r * 8:(r + 1) * 8], axis=0, keepdims=True)
-            parts[r] = jnp.where(sub == i, line, parts[r])
-    y_part[0] = parts[0]
-    y_part[1] = parts[1]
-    remote(y_part.at[other], y_sib, 5, dev(ctx, other)).start()
-    arrived(y_sib, 5)
-    y_send[...] = y_part[core] + y_sib[...]
-    for i in range(1, 8):
-        peer = (group + i) % 8
-        remote(y_send, y_all.at[group], 6, dev(chip_of(peer, colour), core)).start()
-    y_all[group] = y_send[...]
-    arrived(y_all.at[pl.ds(0, 7)], 6)
-    y_sum = y_all[0]
-    for g in range(1, 8):
-        y_sum = y_sum + y_all[g]
-    piece[...] = (resid + y_sum).astype(BF16)
-    for i in range(1, 16):
-        peer = (me_tile + i) % 16
-        remote(piece, out_b.at[me_tile], 7, dev(chip_of(group, peer // 2), peer % 2)).start()
-    out_b[me_tile] = piece[...]
-    arrived(out_b.at[pl.ds(0, 15)], 7)
-    out[...] = out_b[...]
+
+    def y_chunk(part, start, phase, sib):
+        size = part.shape[2]
+        piece_of = lax.broadcasted_iota(jnp.int32, (8, size), 0)
+        sums = [jnp.zeros((8, size), F32), jnp.zeros((8, size), F32)]
+        for i in range(0, 8, 2):
+            cut = jnp.concatenate([wout_s[:, :, k * dspan + start:k * dspan + start + size].reshape(1024, size)
+                                   for k in (i, i + 1)], axis=1)
+            mixed = jnp.dot(spread, cut, preferred_element_type=F32)
+            for k in range(2):
+                for r in range(2):
+                    line = jnp.sum(mixed[r * 8:(r + 1) * 8, k * size:(k + 1) * size], axis=0, keepdims=True)
+                    sums[r] = jnp.where(piece_of == i + k, line, sums[r])
+        part[0] = sums[0]
+        part[1] = sums[1]
+        remote(part.at[other], sib, phase, dev(ctx, other)).start()
+
+    def y_share(part, sib, ysend, yall, swap_phase, phase):
+        arrived(sib, swap_phase)
+        ysend[...] = part[core] + sib[...]
+        for chip, _ in class_chips:
+            remote(ysend, yall.at[group], phase, dev(chip, core)).start()
+        yall[group] = ysend[...]
+
+    def out_share(yall, piece, dest, start, y_phase, phase):
+        arrived(yall.at[pl.ds(0, 7)], y_phase)
+        y_sum = yall[0]
+        for g in range(1, 8):
+            y_sum = y_sum + yall[g]
+        piece[...] = (resid[:, start:start + piece.shape[1]] + y_sum).astype(BF16)
+        for chip, c, _ in tile_peers:
+            remote(piece, dest.at[me_tile], phase, dev(chip, c)).start()
+        dest[me_tile] = piece[...]
+
+    first = part_a.shape[2]
+    y_chunk(part_a, 0, 6, sib_a)
+    y_chunk(part_b, first, 7, sib_b)
+    y_share(part_a, sib_a, ysend_a, yall_a, 6, 8)
+    y_share(part_b, sib_b, ysend_b, yall_b, 7, 9)
+    out_share(yall_a, piece_a, out_a, 0, 8, 10)
+    out_share(yall_b, piece_b, out_b, first, 9, 11)
+    arrived(out_a.at[pl.ds(0, 15)], 10)
+    out[:, :, 0:first] = out_a[...]
+    arrived(out_b.at[pl.ds(0, 15)], 11)
+    out[:, :, first:dspan] = out_b[...]
     left(rs1.at[pl.ds(0, 7)], 0)
     left(lat_b.at[pl.ds(0, 15)], 1)
     left(rope_b.at[pl.ds(0, 15)], 2)
     left(q_all.at[pl.ds(0, 15)], 3)
     left(o_buf.at[pl.ds(0, 15)], 4)
-    left(y_sib, 5)
-    left(y_all.at[pl.ds(0, 7)], 6)
-    left(out_b.at[pl.ds(0, 15)], 7)
+    left(ml_all.at[pl.ds(0, 15)], 5)
+    left(sib_a, 6)
+    left(sib_b, 7)
+    left(yall_a.at[pl.ds(0, 7)], 8)
+    left(yall_b.at[pl.ds(0, 7)], 9)
+    left(out_a.at[pl.ds(0, 15)], 10)
+    left(out_b.at[pl.ds(0, 15)], 11)
 
 
 def solution(mesh):
@@ -280,6 +314,8 @@
         scale = (w_uq.shape[2] + w_qr.shape[2]) ** -0.5
         width = hidden.shape[1]
         dspan = width // 8
+        first = dspan // 128 // 2 * 128 + 128
+        second = dspan - first
         vmem, dma = pltpu.VMEM, pltpu.SemaphoreType.DMA
         anywhere = pl.BlockSpec(memory_space=pl.ANY)
         scratch = [
@@ -303,15 +339,24 @@
             vmem((16, 8, 640), BF16),
             vmem((128, 1024), F32),
             vmem((128, 1024), BF16),
-            vmem((16, 8, 640), F32),
-            vmem((16, 8, 640), F32),
-            vmem((2, 8, dspan), F32),
-            vmem((8, dspan), F32),
-            vmem((8, dspan), F32),
-            vmem((8, 8, dspan), F32),
-            vmem((8, dspan), BF16),
-            vmem((16, 8, dspan), BF16),
-            dma((10,)), dma((2,)), dma((8,)), dma((8,)),
+            vmem((16, 8, 512), F32),
+            vmem((16, 8, 512), F32),
+            vmem((2, 128), F32),
+            vmem((16, 2, 128), F32),
+            vmem((128, 128), F32),
+            vmem((2, 8, first), F32),
+            vmem((2, 8, second), F32),
+            vmem((8, first), F32),
+            vmem((8, second), F32),
+            vmem((8, first), F32),
+            vmem((8, second), F32),
+            vmem((8, 8, first), F32),
+            vmem((8, 8, second), F32),
+            vmem((8, first), BF16),
+            vmem((8, second), BF16),
+            vmem((16, 8, first), BF16),
+            vmem((16, 8, second), BF16),
+            dma((10,)), dma((2,)), dma((12,)), dma((12,)),
         ]
         out = pl.pallas_call(
             functools.partial(kernel, scale),

time: 46.2 us -> 44.6 us (0.965)
  Pallas kernels: 44.4 us -> 42.9 us
    pallas_call x1, Pallas kernels: 44.4 us -> 42.9 us  [local_step(): pl.pallas_call(functools.partial(kernel, scale), out_shape=jax.ShapeDtype...]
where the time goes in v3:
time: 44.6 us; the launch traced here: 44.5 us
  Pallas kernels  42.9 us (96%)
  local copies, waits for them, and re-layouts  1.6 us (4%)
    pallas_call x1, Pallas kernels, local_step(): pl.pallas_call(functools.partial(kernel, scale), out_shape=jax.ShapeDtype...  42.9 us
    unnamed x1, local copies, waits for them, and re-layouts  1.6 us

profile of v3, /device:TPU:1, one launch (start us, length us, event | category | flops | bytes accessed | tf_op | source)
XLA Modules:
  0.0 44.5 jit_solution(18116005007573151163)
XLA Ops:
  0.0 42.9 %mla_decode.1 = bf16[16,8,640]{2,1,0:T(8,128)(2,1)} custom-call(bf16[2,8,5120]{2,1,0:T(8,128)(2,1)} %bitcast.6, s32[16]{0:T(128)} %lengths.1, bf16[16,64,512]{2,1,0:T(8,128)(2,1)} %latent.1, bf16[16,64,64]{2,1,0:T(8,128)(2,1)} %rope.1, bf16[5120,64,128]{2,1,0:T(8,128)(2,1)} %wuq.1, bf16[64,64,5120]{2,1,0:T(8,128)(2,1)} %bitcast.4, ...), custom_call_target="tpu_custom_call" | custom-call | tf_op jit(solution)/shard_map/mla_decode/pallas_call | solution.py:361
  42.9 1.6 %copy.10 = bf16[2,8,8,640]{3,1,2,0:T(8,128)(2,1)} copy(bf16[2,8,8,640]{3,2,1,0:T(8,128)(2,1)} %bitcast.5) | data formatting | bytes 327680

commit v4 on v3

--- a/solution.py
+++ b/solution.py
@@ -18,13 +18,16 @@
 
 
 CLASS = ((2, 2, 0), (0, 2, 2), (2, 0, 2), (1, 2, 1), (3, 2, 3), (1, 0, 3), (3, 0, 1))
+NEAR = ((0, 1, 0), (0, 3, 0), (0, 0, 1), (0, 0, 3), (1, 0, 1), (3, 0, 3), (1, 3, 0), (3, 1, 0), (0, 1, 1), (0, 3, 3),
+        (1, 1, 0), (3, 3, 0))
+RELAY = ((0, 1, 1), (0, 3, 3), (1, 0, 1), (1, 3, 0), (1, 0, 0), (3, 0, 0))
 
 
 def kernel(scale, hidden, lengths, latent, rope, wuq, wqr, wuk, wuv, wout, out,
            len_s, hid_s, hid_r, wq_s, wq_f, wr_s, wuk_s, wuv_s, wout_s, lat_s, rope_s, rope_p,
            lat_b, rope_b, qp, rs1, q_send, q_all, s_buf, p_buf, acc_send, o_buf, ml_send, ml_all, ml_t,
            part_a, part_b, sib_a, sib_b, ysend_a, ysend_b, yall_a, yall_b, piece_a, piece_b, out_a, out_b,
-           load_sem, own_sem, send_sem, recv_sem):
+           load_sem, own_sem, send_sem, recv_sem, near_sem):
     ctx = lax.axis_index('ctx')
     core = lax.axis_index('seq')
     z, y, x = ctx // 16, (ctx // 4) % 4, ctx % 4
@@ -93,14 +96,12 @@
     for d in (1, 3):
         tile_chips.append((zs16[0] + ys4[0] + xs[d], (xs[d] + y + z) % 4 + 4 * (y % 2)))
     tile_peers = [(chip, c, j) for chip, j in tile_chips for c in range(2)] + [(ctx, other, colour)]
-    for chip, c, _ in class_peers[:-1]:
-        greet(chip, c)
+    sources = [chip_at(o, -1) for o in SHIFTS]
     for chip, c, _ in tile_peers:
         greet(chip, c)
-    sources = [chip_at(o, -1) for o in SHIFTS]
-    for t in (5, 6, 7, 1, 2, 3, 4):
+    for offset in NEAR:
         for c in range(2):
-            greet(sources[t], c)
+            greet(chip_at(offset), c)
 
     loads[0].wait()
     chunk = 64
@@ -126,7 +127,9 @@
         rope_p[b] = jnp.concatenate([rope_s[b, 0:32, :], rope_s[b, 32:64, :]], axis=1)
     loads[3].wait()
 
-    pl.semaphore_wait(barrier, 43)
+    pl.semaphore_wait(barrier, 39)
+    for offset in RELAY:
+        pl.semaphore_signal(near_sem, inc=1, device_id=dev(chip_at(offset), core), device_id_type=pl.DeviceIdType.MESH)
 
     def pair_rows(c):
         return pl.ds(pl.multiple_of(c * 16, 16), 16)
@@ -134,18 +137,18 @@
     for chip, peer in tile_chips:
         remote(qp.at[:, pair_rows(peer), :], rs1.at[colour], 0, dev(chip, core)).start()
 
-    def cache_send(t, c):
+    def cache_send(t, c, late):
         chip = chip_at(SHIFTS[t])
         target = (colour + STEPS[t][0]) % 4 + 4 * ((colour // 4 + STEPS[t][1]) % 2)
         src_row = 2 * target + c
         slot = 2 * t + core
-        remote(lat_s.at[src_row], lat_b.at[slot], 1, dev(chip, c)).start()
-        remote(rope_p.at[src_row], rope_b.at[slot], 2, dev(chip, c)).start()
+        remote(lat_s.at[src_row], lat_b.at[slot], 12 if late else 1, dev(chip, c)).start()
+        remote(rope_p.at[src_row], rope_b.at[slot], 13 if late else 2, dev(chip, c)).start()
 
     for t in (5, 6, 7):
         for c in range(2):
-            cache_send(t, c)
-    cache_send(0, other)
+            cache_send(t, c, False)
+    cache_send(0, other, False)
     own_l = pltpu.make_async_copy(lat_s.at[row], lat_b.at[core], own_sem.at[0])
     own_r = pltpu.make_async_copy(rope_p.at[row], rope_b.at[core], own_sem.at[1])
     own_l.start()
@@ -169,11 +172,12 @@
     for r in range(2):
         q_send[r, :, 0:512] = q_lat[r * 8:(r + 1) * 8].astype(BF16)
         q_send[r, :, 512:640] = q_rope[r * 8:(r + 1) * 8].astype(BF16)
+    pl.semaphore_wait(near_sem, 6)
     for chip, c, _ in class_peers:
         remote(q_send.at[c], q_all.at[me_class], 3, dev(chip, c)).start()
     for t in range(1, 5):
         for c in range(2):
-            cache_send(t, c)
+            cache_send(t, c, True)
     q_all[me_class] = q_send[core]
 
     loads[8].wait()
@@ -191,12 +195,12 @@
     own_l.wait()
     own_r.wait()
     arrived(q_all.at[pl.ds(0, 15)], 3)
-    arrived(lat_b.at[pl.ds(0, 15)], 1)
-    arrived(rope_b.at[pl.ds(0, 15)], 2)
+    arrived(lat_b.at[pl.ds(0, 7)], 1)
+    arrived(rope_b.at[pl.ds(0, 7)], 2)
     queries = q_all[...].astype(F32).reshape(128, 640).astype(BF16)
     lane = lax.broadcasted_iota(jnp.int32, (128, 128), 1)
-    top = None
-    for t in range(8):
+
+    def scores(t):
         keys = lat_b[2 * t:2 * t + 2].reshape(128, 512)
         packed = rope_b[2 * t:2 * t + 2]
         rkeys = jnp.concatenate([packed[:, :, 0:64], packed[:, :, 64:128]], axis=1).reshape(128, 64)
@@ -204,17 +208,21 @@
         s = (s + lax.dot_general(queries[:, 512:576], rkeys, NT, preferred_element_type=F32)) * scale
         s = jnp.where(sources[t] * 128 + lane < length, s, NEG_FILL)
         s_buf[:, t * 128:(t + 1) * 128] = s
-        m_t = jnp.max(s, axis=1, keepdims=True)
-        top = m_t if top is None else jnp.maximum(top, m_t)
+        return jnp.max(s, axis=1, keepdims=True)
+
+    top = functools.reduce(jnp.maximum, [scores(t) for t in (0, 5, 6, 7)])
+    arrived(lat_b.at[pl.ds(0, 8)], 12)
+    arrived(rope_b.at[pl.ds(0, 8)], 13)
+    top = functools.reduce(jnp.maximum, [top] + [scores(t) for t in range(1, 5)])
     den = jnp.zeros((128, 1), F32)
     for t in range(8):
         valid = sources[t] * 128 + lane < length
         w = jnp.where(valid, jnp.exp(s_buf[:, t * 128:(t + 1) * 128] - top), 0.0)
         den = den + jnp.sum(w, axis=1, keepdims=True)
         p_buf[:, t * 128:(t + 1) * 128] = w.astype(BF16)
+    ml_send[...] = jnp.where(lane == 0, top, den).T[0:2]
     acc = jnp.dot(p_buf[...], lat_b[...].reshape(1024, 512), preferred_element_type=F32)
     acc_send[...] = acc.reshape(16, 8, 512)
-    ml_send[...] = jnp.where(lane == 0, top, den).T[0:2]
 
     for chip, c, _ in class_peers:
         remote(ml_send, ml_all.at[me_class], 5, dev(chip, c)).start()
@@ -225,18 +233,23 @@
     arrived(ml_all.at[pl.ds(0, 15)], 5)
     ml_t[:, 0:32] = ml_all[...].reshape(32, 128).T
     ml = ml_t[pl.ds(pl.multiple_of(me_class * 8, 8), 8), :]
+    factors, dens = [], []
+    for r in range(2):
+        m_all = [ml[:, 2 * (r * 8 + g):2 * (r * 8 + g) + 1] for g in range(8)]
+        best = functools.reduce(jnp.maximum, m_all)
+        den_r = jnp.zeros((8, 1), F32)
+        for g in range(8):
+            factor = jnp.exp(m_all[g] - best)
+            den_r = den_r + ml[:, 2 * (r * 8 + g) + 1:2 * (r * 8 + g) + 2] * factor
+            factors.append(jnp.broadcast_to(factor, (8, 512)))
+        dens.append(den_r)
     arrived(o_buf.at[pl.ds(0, 15)], 4)
     finished = []
     for r in range(2):
-        m_all = [ml[:, 2 * (r * 8 + g):2 * (r * 8 + g) + 1] for g in range(8)]
-        best = functools.reduce(jnp.maximum, m_all)
         num = jnp.zeros((8, 512), F32)
-        den_r = jnp.zeros((8, 1), F32)
         for g in range(8):
-            factor = jnp.exp(m_all[g] - best)
-            num = num + o_buf[r * 8 + g] * factor
-            den_r = den_r + ml[:, 2 * (r * 8 + g) + 1:2 * (r * 8 + g) + 2] * factor
-        finished.append(num / den_r)
+            num = num + o_buf[r * 8 + g] * factors[r * 8 + g]
+        finished.append(num / dens[r])
     o_lat = jnp.concatenate(finished, axis=0).astype(BF16)
     row_head = lax.broadcasted_iota(jnp.int32, (16, 128), 0) % 8
     vals = jnp.zeros((16, 128), F32)
@@ -291,8 +304,10 @@
     arrived(out_b.at[pl.ds(0, 15)], 11)
     out[:, :, first:dspan] = out_b[...]
     left(rs1.at[pl.ds(0, 7)], 0)
-    left(lat_b.at[pl.ds(0, 15)], 1)
-    left(rope_b.at[pl.ds(0, 15)], 2)
+    left(lat_b.at[pl.ds(0, 7)], 1)
+    left(rope_b.at[pl.ds(0, 7)], 2)
+    left(lat_b.at[pl.ds(0, 8)], 12)
+    left(rope_b.at[pl.ds(0, 8)], 13)
     left(q_all.at[pl.ds(0, 15)], 3)
     left(o_buf.at[pl.ds(0, 15)], 4)
     left(ml_all.at[pl.ds(0, 15)], 5)
@@ -356,7 +371,7 @@
             vmem((8, second), BF16),
             vmem((16, 8, first), BF16),
             vmem((16, 8, second), BF16),
-            dma((10,)), dma((2,)), dma((12,)), dma((12,)),
+            dma((10,)), dma((2,)), dma((14,)), dma((14,)), pltpu.SemaphoreType.REGULAR,
         ]
         out = pl.pallas_call(
             functools.partial(kernel, scale),

time: 44.6 us -> 44 us (0.987)
  Pallas kernels: 42.9 us -> 42.3 us
    pallas_call x1, Pallas kernels: 42.9 us -> 42.3 us  [local_step(): pl.pallas_call(functools.partial(kernel, scale), out_shape=jax.ShapeDtype...]
where the time goes in v4:
time: 44 us; the launch traced here: 43.9 us
  Pallas kernels  42.3 us (96%)
  local copies, waits for them, and re-layouts  1.6 us (4%)
    pallas_call x1, Pallas kernels, local_step(): pl.pallas_call(functools.partial(kernel, scale), out_shape=jax.ShapeDtype...  42.3 us
    unnamed x1, local copies, waits for them, and re-layouts  1.6 us

profile of v4, /device:TPU:1, one launch (start us, length us, event | category | flops | bytes accessed | tf_op | source)
XLA Modules:
  0.0 43.9 jit_solution(17059649503792925103)
XLA Ops:
  0.0 42.3 %mla_decode.1 = bf16[16,8,640]{2,1,0:T(8,128)(2,1)} custom-call(bf16[2,8,5120]{2,1,0:T(8,128)(2,1)} %bitcast.6, s32[16]{0:T(128)} %lengths.1, bf16[16,64,512]{2,1,0:T(8,128)(2,1)} %latent.1, bf16[16,64,64]{2,1,0:T(8,128)(2,1)} %rope.1, bf16[5120,64,128]{2,1,0:T(8,128)(2,1)} %wuq.1, bf16[64,64,5120]{2,1,0:T(8,128)(2,1)} %bitcast.4, ...), custom_call_target="tpu_custom_call" | custom-call | tf_op jit(solution)/shard_map/mla_decode/pallas_call | solution.py:376
  42.3 1.6 %copy.10 = bf16[2,8,8,640]{3,1,2,0:T(8,128)(2,1)} copy(bf16[2,8,8,640]{3,2,1,0:T(8,128)(2,1)} %bitcast.5) | data formatting | bytes 327680

commit v5 on v4

--- a/solution.py
+++ b/solution.py
@@ -26,7 +26,7 @@
 def kernel(scale, hidden, lengths, latent, rope, wuq, wqr, wuk, wuv, wout, out,
            len_s, hid_s, hid_r, wq_s, wq_f, wr_s, wuk_s, wuv_s, wout_s, lat_s, rope_s, rope_p,
            lat_b, rope_b, qp, rs1, q_send, q_all, s_buf, p_buf, acc_send, o_buf, ml_send, ml_all, ml_t,
-           part_a, part_b, sib_a, sib_b, ysend_a, ysend_b, yall_a, yall_b, piece_a, piece_b, out_a, out_b,
+           part_a, part_b, sib_a, sib_b, ysend_a, ysend_b, yall_a, yall_b, piece_a, piece_b, out_a, out_b, rows_f,
            load_sem, own_sem, send_sem, recv_sem, near_sem):
     ctx = lax.axis_index('ctx')
     core = lax.axis_index('seq')
@@ -299,10 +299,20 @@
     y_share(part_b, sib_b, ysend_b, yall_b, 7, 9)
     out_share(yall_a, piece_a, out_a, 0, 8, 10)
     out_share(yall_b, piece_b, out_b, first, 9, 11)
+
+    def place(pieces, start):
+        for tile in range(pieces.shape[2] // 128):
+            rows_f[...] = pieces[:, :, tile * 128:(tile + 1) * 128].astype(F32).reshape(128, 128)
+            for i in range(8):
+                lanes = pl.ds(i * dspan + start + tile * 128, 128)
+                rows = rows_f[pl.ds(i, 16, stride=8), :]
+                out[0, :, lanes] = rows[0:8].astype(BF16)
+                out[1, :, lanes] = rows[8:16].astype(BF16)
+
     arrived(out_a.at[pl.ds(0, 15)], 10)
-    out[:, :, 0:first] = out_a[...]
+    place(out_a, 0)
     arrived(out_b.at[pl.ds(0, 15)], 11)
-    out[:, :, first:dspan] = out_b[...]
+    place(out_b, first)
     left(rs1.at[pl.ds(0, 7)], 0)
     left(lat_b.at[pl.ds(0, 7)], 1)
     left(rope_b.at[pl.ds(0, 7)], 2)
@@ -317,6 +327,12 @@
     left(yall_b.at[pl.ds(0, 7)], 9)
     left(out_a.at[pl.ds(0, 15)], 10)
     left(out_b.at[pl.ds(0, 15)], 11)
+
+
+def finish(rows, out, sem):
+    copy = pltpu.make_async_copy(rows, out, sem)
+    copy.start()
+    copy.wait()
 
 
 def solution(mesh):
@@ -371,20 +387,29 @@
             vmem((8, second), BF16),
             vmem((16, 8, first), BF16),
             vmem((16, 8, second), BF16),
+            vmem((128, 128), F32),
             dma((10,)), dma((2,)), dma((14,)), dma((14,)), pltpu.SemaphoreType.REGULAR,
         ]
         out = pl.pallas_call(
             functools.partial(kernel, scale),
-            out_shape=jax.ShapeDtypeStruct((16, 8, dspan), BF16),
+            out_shape=vmem((2, 8, width), BF16),
             in_specs=[anywhere] * 9,
             out_specs=pl.BlockSpec(memory_space=pltpu.VMEM),
             scratch_shapes=scratch,
             compiler_params=pltpu.CompilerParams(collective_id=0, has_side_effects=True,
-                                                 vmem_limit_bytes=67043328),
+                                                 vmem_limit_bytes=60 * 1024 * 1024),
             name='mla_decode',
         )(hidden.reshape(2, 8, width), lengths, latent_cache, rope_keys, w_uq,
           jnp.transpose(w_qr, (1, 2, 0)), w_uk, w_uv, w_out)
-        return out.reshape(16, width)
+        done = pl.pallas_call(
+            finish,
+            out_shape=jax.ShapeDtypeStruct((2, 8, width), BF16),
+            in_specs=[pl.BlockSpec(memory_space=pltpu.VMEM)],
+            out_specs=pl.BlockSpec(memory_space=pl.ANY),
+            scratch_shapes=[dma],
+            name='mla_out',
+        )(pltpu.with_memory_space_constraint(out, pltpu.VMEM))
+        return done.reshape(16, width)
 
     return jax.shard_map(local_step, mesh=mesh,
                          in_specs=(row_spec, P('batch'), cache_spec, cache_spec, proj_spec, proj_spec, head_spec, head_spec, head_spec),

time: 44 us -> 42.2 us (0.959)
  local copies, waits for them, and re-layouts: 1.6 us -> 0 us
    unnamed x1 -> x0, local copies, waits for them, and re-layouts: 1.6 us -> none
    pallas_call x1 -> x2, Pallas kernels: 42.3 us -> 42.1 us  [the longest x1 41.4 us: local_step(): pl.pallas_call(functools.partial(kernel, scale), out_shape=vmem((2, 8, wi...]
where the time goes in v5:
time: 42.2 us; the launch traced here: 42.1 us
  Pallas kernels  42.1 us (100%)
    pallas_call x1, Pallas kernels, local_step(): pl.pallas_call(functools.partial(kernel, scale), out_shape=vmem((2, 8, wi...  41.4 us

profile of v5, /device:TPU:1, one launch (start us, length us, event | category | flops | bytes accessed | tf_op | source)
XLA Modules:
  0.0 42.1 jit_solution(10338751430649152729)
XLA Ops:
  0.0 41.4 %mla_decode.1.rows = bf16[2,8,5120]{2,1,0:T(8,128)(2,1)S(1)} custom-call(bf16[2,8,5120]{2,1,0:T(8,128)(2,1)} %bitcast.4, s32[16]{0:T(128)} %lengths.1, bf16[16,64,512]{2,1,0:T(8,128)(2,1)} %latent.1, bf16[16,64,64]{2,1,0:T(8,128)(2,1)} %rope.1, bf16[5120,64,128]{2,1,0:T(8,128)(2,1)} %wuq.1, bf16[64,64,5120]{2,1,0:T(8,128)(2,1)} %bitcast.3, ...), custom_call_target="tpu_custom_call" | custom-call | tf_op jit(solution)/shard_map/mla_decode/pallas_call | solution.py:393
  41.4 0.7 %mla_out.1 = bf16[2,8,5120]{2,1,0:T(8,128)(2,1)} custom-call(bf16[2,8,5120]{2,1,0:T(8,128)(2,1)S(1)} %mla_decode.1.rows), custom_call_target="tpu_custom_call" | custom-call | tf_op jit(solution)/shard_map/mla_out/pallas_call | solution.py:404

commit v6 on v5

v6 whole, which is shorter than its diff:
```python
import functools

import jax
import jax.numpy as jnp
from jax import lax
from jax.experimental import pallas as pl
from jax.experimental.pallas import tpu as pltpu
from jax.sharding import PartitionSpec as P

NEG_FILL = -1.0e30
F32 = jnp.float32
BF16 = jnp.bfloat16

SHIFTS = ((0, 0, 0), (1, 0, 0), (0, 0, -1), (0, 1, 0), (0, -1, 0), (-1, 0, -1), (1, -1, 0), (0, 1, 1))
STEPS = ((0, 0), (1, 0), (3, 0), (1, 1), (3, 1), (2, 0), (0, 1), (2, 1))

LANES, LATENT, ROWS, OCT, HALF, WIDE, QWIDE, HALVED, PEERS, CHIPS = 128, 512, 16, 8, 64, 1024, 640, 32, 15, 7
NT = (((1,), (1,)), ((), ()))


CLASS = ((2, 2, 0), (0, 2, 2), (2, 0, 2), (1, 2, 1), (3, 2, 3), (1, 0, 3), (3, 0, 1))
NEAR = ((0, 1, 0), (0, 3, 0), (0, 0, 1), (0, 0, 3), (1, 0, 1), (3, 0, 3), (1, 3, 0), (3, 1, 0), (0, 1, 1), (0, 3, 3),
        (1, 1, 0), (3, 3, 0))
RELAY = ((0, 1, 1), (0, 3, 3), (1, 0, 1), (1, 3, 0), (1, 0, 0), (3, 0, 0))


def kernel(scale, hidden, lengths, latent, rope, wuq, wqr, wuk, wuv, wout, out,
           len_s, hid_s, hid_r, wq_s, wq_f, wr_s, wuk_s, wuv_s, wout_s, lat_s, rope_s, rope_p,
           lat_b, rope_b, qp, rs1, q_send, q_all, s_buf, p_buf, acc_send, o_buf, ml_send, ml_all, ml_t,
           part_a, part_b, sib_a, sib_b, ysend_a, ysend_b, yall_a, yall_b, piece_a, piece_b, out_a, out_b, rows_f,
           load_sem, own_sem, send_sem, recv_sem, near_sem):
    ctx = lax.axis_index('ctx')
    core = lax.axis_index('seq')
    z, y, x = ctx // ROWS, (ctx // 4) % 4, ctx % 4
    xs = [(x + d) % 4 for d in range(4)]
    ys = [(y + d) % 4 for d in range(4)]
    zs = [(z + d) % 4 for d in range(4)]
    ys4 = [v * 4 for v in ys]
    zs16 = [v * ROWS for v in zs]

    def chip_at(offset, sign=1):
        dx, dy, dz = offset
        return zs16[sign * dz % 4] + ys4[sign * dy % 4] + xs[sign * dx % 4]

    colour = (x + y + z) % 4 + 4 * (y % 2)
    group = z * 2 + y // 2
    other = 1 - core
    row = 2 * colour + core
    dspan = hid_s.shape[2]
    cols = pl.ds(pl.multiple_of(colour * dspan, LANES), dspan)
    heads = pl.ds(pl.multiple_of(group * OCT, OCT), OCT)

    def dev(chip, c):
        return (0, chip, c)

    def remote(src, dst, phase, device):
        return pltpu.make_async_remote_copy(src_ref=src, dst_ref=dst, send_sem=send_sem.at[phase],
                                            recv_sem=recv_sem.at[phase], device_id=device,
                                            device_id_type=pl.DeviceIdType.MESH)

    def arrived(part, phase):
        remote(part, part, phase, dev(ctx, other)).wait_recv()

    def left(part, phase):
        remote(part, part, phase, dev(ctx, other)).wait_send()

    loads = [
        pltpu.make_async_copy(wuq.at[pl.ds(pl.multiple_of(colour * dspan, LANES), dspan), heads, :], wq_s, load_sem.at[0]),
        pltpu.make_async_copy(wqr.at[heads, :, cols], wr_s, load_sem.at[1]),
        pltpu.make_async_copy(hidden.at[:, :, cols], hid_s, load_sem.at[2]),
        pltpu.make_async_copy(latent, lat_s, load_sem.at[3]),
        pltpu.make_async_copy(rope, rope_s, load_sem.at[4]),
        pltpu.make_async_copy(wuk.at[heads], wuk_s, load_sem.at[5]),
        pltpu.make_async_copy(wuv.at[heads], wuv_s, load_sem.at[6]),
        pltpu.make_async_copy(wout.at[heads], wout_s, load_sem.at[CHIPS]),
        pltpu.make_async_copy(lengths, len_s, load_sem.at[OCT]),
        pltpu.make_async_copy(hidden.at[row // OCT], hid_r, load_sem.at[9]),
    ]
    for i in (0, 1, 2, 4, 3, 5):
        loads[i].start()

    barrier = pltpu.get_barrier_semaphore()

    def greet(chip, c):
        pl.semaphore_signal(barrier, inc=1, device_id=dev(chip, c), device_id_type=pl.DeviceIdType.MESH)

    me_class = core * OCT + group
    me_tile = colour * 2 + core
    class_chips = [(chip_at(o), zs[o[2]] * 2 + ys[o[1]] // 2) for o in CLASS]
    class_peers = [(chip, c, c * OCT + g) for chip, g in class_chips for c in range(2)] + [(ctx, other, other * OCT + group)]
    mate = y + 1 - 2 * (y % 2)
    tile_chips = []
    for d in (2, 1, 3):
        tile_chips.append((z * ROWS + mate * 4 + xs[d], (xs[d] + mate + z) % 4 + 4 * (mate % 2)))
    tile_chips.append((zs16[0] + ys4[0] + xs[2], (xs[2] + y + z) % 4 + 4 * (y % 2)))
    tile_chips.append((z * ROWS + mate * 4 + x, (x + mate + z) % 4 + 4 * (mate % 2)))
    for d in (1, 3):
        tile_chips.append((zs16[0] + ys4[0] + xs[d], (xs[d] + y + z) % 4 + 4 * (y % 2)))
    tile_peers = [(chip, c, j) for chip, j in tile_chips for c in range(2)] + [(ctx, other, colour)]
    sources = [chip_at(o, -1) for o in SHIFTS]
    for chip, c, _ in tile_peers:
        greet(chip, c)
    for offset in NEAR:
        for c in range(2):
            greet(chip_at(offset), c)

    loads[0].wait()
    chunk = HALF

    @pl.loop(0, dspan // chunk)
    def _(i):
        rows = wq_s[pl.ds(i * chunk, chunk)].astype(F32).reshape(chunk * OCT, LANES)
        wq_f[pl.ds(pl.multiple_of(i * chunk * OCT, OCT), chunk * OCT), :] = rows

    loads[1].wait()
    loads[2].wait()
    hid = hid_s[...].astype(F32).reshape(ROWS, dspan).astype(BF16)
    w_n = jnp.concatenate([wq_f[pl.ds(h, dspan, stride=OCT), :].astype(BF16) for h in range(OCT)], axis=1)
    part_n = jnp.dot(hid, w_n, preferred_element_type=F32)
    for h in range(OCT):
        qp[0, pl.ds(h, ROWS, stride=OCT), :] = part_n[:, h * LANES:(h + 1) * LANES]
    part_r = lax.dot_general(hid, wr_s[...].reshape(LATENT, dspan), NT, preferred_element_type=F32)
    for pair in range(4):
        both = part_r[:, pair * LANES:(pair + 1) * LANES]
        qp[1, pl.ds(2 * pair, ROWS, stride=OCT), :] = both
        qp[1, pl.ds(2 * pair + 1, ROWS, stride=OCT), :] = pltpu.roll(both, HALF, 1)
    loads[4].wait()
    for b in range(ROWS):
        rope_p[b] = jnp.concatenate([rope_s[b, 0:HALVED, :], rope_s[b, HALVED:HALF, :]], axis=1)
    loads[3].wait()

    pl.semaphore_wait(barrier, 39)
    for offset in RELAY:
        pl.semaphore_signal(near_sem, inc=1, device_id=dev(chip_at(offset), core), device_id_type=pl.DeviceIdType.MESH)

    def pair_rows(c):
        return pl.ds(pl.multiple_of(c * ROWS, ROWS), ROWS)

    for chip, peer in tile_chips:
        remote(qp.at[:, pair_rows(peer), :], rs1.at[colour], 0, dev(chip, core)).start()

    def cache_send(t, c, late):
        chip = chip_at(SHIFTS[t])
        target = (colour + STEPS[t][0]) % 4 + 4 * ((colour // 4 + STEPS[t][1]) % 2)
        src_row = 2 * target + c
        slot = 2 * t + core
        remote(lat_s.at[src_row], lat_b.at[slot], 12 if late else 1, dev(chip, c)).start()
        remote(rope_p.at[src_row], rope_b.at[slot], 13 if late else 2, dev(chip, c)).start()

    for t in (5, 6, CHIPS):
        for c in range(2):
            cache_send(t, c, False)
    cache_send(0, other, False)
    own_l = pltpu.make_async_copy(lat_s.at[row], lat_b.at[core], own_sem.at[0])
    own_r = pltpu.make_async_copy(rope_p.at[row], rope_b.at[core], own_sem.at[1])
    own_l.start()
    own_r.start()
    rs1[colour] = qp[:, pair_rows(colour), :]

    for i in (6, CHIPS, OCT, 9):
        loads[i].start()
    loads[5].wait()
    arrived(rs1.at[pl.ds(0, CHIPS)], 0)
    total = rs1[0]
    for i in range(1, OCT):
        total = total + rs1[i]
    row_head = lax.broadcasted_iota(jnp.int32, (ROWS, LANES), 0) % OCT
    q_nope = jnp.concatenate([jnp.where(row_head == h, total[0], 0.0) for h in range(OCT)], axis=1).astype(BF16)
    q_rope = jnp.where(lax.broadcasted_iota(jnp.int32, (ROWS, LANES), 1) < HALF, total[1], 0.0)
    q_lat = jnp.dot(q_nope, wuk_s[...].reshape(WIDE, LATENT), preferred_element_type=F32)
    for r in range(2):
        q_send[r, :, 0:LATENT] = q_lat[r * OCT:(r + 1) * OCT].astype(BF16)
        q_send[r, :, LATENT:QWIDE] = q_rope[r * OCT:(r + 1) * OCT].astype(BF16)
    pl.semaphore_wait(near_sem, 6)
    for chip, c, _ in class_peers:
        remote(q_send.at[c], q_all.at[me_class], 3, dev(chip, c)).start()
    for t in range(1, 5):
        for c in range(2):
            cache_send(t, c, True)
    q_all[me_class] = q_send[core]

    loads[OCT].wait()
    loads[9].wait()
    length = len_s[row]
    sub = lax.broadcasted_iota(jnp.int32, (OCT, dspan), 0)
    resid = jnp.zeros((OCT, dspan), F32)
    for i in range(OCT):
        block = hid_r[:, i * dspan:(i + 1) * dspan].astype(F32)
        line = jnp.sum(jnp.where(sub == row % OCT, block, 0.0), axis=0, keepdims=True)
        resid = jnp.where(sub == i, line, resid)
    loads[6].wait()
    loads[CHIPS].wait()

    own_l.wait()
    own_r.wait()
    arrived(q_all.at[pl.ds(0, PEERS)], 3)
    arrived(lat_b.at[pl.ds(0, CHIPS)], 1)
    arrived(rope_b.at[pl.ds(0, CHIPS)], 2)
    queries = q_all[...].astype(F32).reshape(LANES, QWIDE).astype(BF16)
    lane = lax.broadcasted_iota(jnp.int32, (LANES, LANES), 1)

    def scores(t):
        keys = lat_b[2 * t:2 * t + 2].reshape(LANES, LATENT)
        packed = rope_b[2 * t:2 * t + 2]
        rkeys = jnp.concatenate([packed[:, :, 0:HALF], packed[:, :, HALF:LANES]], axis=1).reshape(LANES, HALF)
        s = lax.dot_general(queries[:, 0:LATENT], keys, NT, preferred_element_type=F32)
        s = (s + lax.dot_general(queries[:, LATENT:576], rkeys, NT, preferred_element_type=F32)) * scale
        s = jnp.where(sources[t] * LANES + lane < length, s, NEG_FILL)
        s_buf[:, t * LANES:(t + 1) * LANES] = s
        return jnp.max(s, axis=1, keepdims=True)

    top = functools.reduce(jnp.maximum, [scores(t) for t in (0, 5, 6, CHIPS)])
    arrived(lat_b.at[pl.ds(0, OCT)], 12)
    arrived(rope_b.at[pl.ds(0, OCT)], 13)
    top = functools.reduce(jnp.maximum, [top] + [scores(t) for t in range(1, 5)])
    den = jnp.zeros((LANES, 1), F32)
    for t in range(OCT):
        valid = sources[t] * LANES + lane < length
        w = jnp.where(valid, jnp.exp(s_buf[:, t * LANES:(t + 1) * LANES] - top), 0.0)
        den = den + jnp.sum(w, axis=1, keepdims=True)
        p_buf[:, t * LANES:(t + 1) * LANES] = w.astype(BF16)
    ml_send[...] = jnp.where(lane == 0, top, den).T[0:2]
    acc = jnp.dot(p_buf[...], lat_b[...].reshape(WIDE, LATENT), preferred_element_type=F32)
    acc_send[...] = acc.reshape(ROWS, OCT, LATENT)

    for chip, c, _ in class_peers:
        remote(ml_send, ml_all.at[me_class], 5, dev(chip, c)).start()
    for chip, c, peer in class_peers:
        remote(acc_send.at[peer], o_buf.at[me_class], 4, dev(chip, c)).start()
    o_buf[me_class] = acc_send[me_class]
    ml_all[me_class] = ml_send[...]
    arrived(ml_all.at[pl.ds(0, PEERS)], 5)
    ml_t[:, 0:HALVED] = ml_all[...].reshape(HALVED, LANES).T
    ml = ml_t[pl.ds(pl.multiple_of(me_class * OCT, OCT), OCT), :]
    factors, dens = [], []
    for r in range(2):
        m_all = [ml[:, 2 * (r * OCT + g):2 * (r * OCT + g) + 1] for g in range(OCT)]
        best = functools.reduce(jnp.maximum, m_all)
        den_r = jnp.zeros((OCT, 1), F32)
        for g in range(OCT):
            factor = jnp.exp(m_all[g] - best)
            den_r = den_r + ml[:, 2 * (r * OCT + g) + 1:2 * (r * OCT + g) + 2] * factor
            factors.append(jnp.broadcast_to(factor, (OCT, LATENT)))
        dens.append(den_r)
    arrived(o_buf.at[pl.ds(0, PEERS)], 4)
    finished = []
    for r in range(2):
        num = jnp.zeros((OCT, LATENT), F32)
        for g in range(OCT):
            num = num + o_buf[r * OCT + g] * factors[r * OCT + g]
        finished.append(num / dens[r])
    o_lat = jnp.concatenate(finished, axis=0).astype(BF16)
    w_v = jnp.concatenate([wuv_s[h] for h in range(OCT)], axis=1)
    every = jnp.dot(o_lat, w_v, preferred_element_type=F32)
    vals = jnp.zeros((ROWS, LANES), F32)
    for h in range(OCT):
        vals = jnp.where(row_head == h, every[:, h * LANES:(h + 1) * LANES], vals)

    spread = jnp.concatenate([jnp.where(row_head == h, vals, 0.0) for h in range(OCT)], axis=1).astype(BF16)

    def y_chunk(part, start, phase, sib):
        size = part.shape[2]
        piece_of = lax.broadcasted_iota(jnp.int32, (OCT, size), 0)
        sums = [jnp.zeros((OCT, size), F32), jnp.zeros((OCT, size), F32)]
        for i in range(0, OCT, 2):
            cut = jnp.concatenate([wout_s[:, :, k * dspan + start:k * dspan + start + size].reshape(WIDE, size)
                                   for k in (i, i + 1)], axis=1)
            mixed = jnp.dot(spread, cut, preferred_element_type=F32)
            for k in range(2):
                for r in range(2):
                    line = jnp.sum(mixed[r * OCT:(r + 1) * OCT, k * size:(k + 1) * size], axis=0, keepdims=True)
                    sums[r] = jnp.where(piece_of == i + k, line, sums[r])
        part[0] = sums[0]
        part[1] = sums[1]
        remote(part.at[other], sib, phase, dev(ctx, other)).start()

    def y_share(part, sib, ysend, yall, swap_phase, phase):
        arrived(sib, swap_phase)
        ysend[...] = part[core] + sib[...]
        for chip, _ in class_chips:
            remote(ysend, yall.at[group], phase, dev(chip, core)).start()
        yall[group] = ysend[...]

    def out_share(yall, piece, dest, start, y_phase, phase):
        arrived(yall.at[pl.ds(0, CHIPS)], y_phase)
        y_sum = yall[0]
        for g in range(1, OCT):
            y_sum = y_sum + yall[g]
        piece[...] = (resid[:, start:start + piece.shape[1]] + y_sum).astype(BF16)
        for chip, c, _ in tile_peers:
            remote(piece, dest.at[me_tile], phase, dev(chip, c)).start()
        dest[me_tile] = piece[...]

    first = part_a.shape[2]
    y_chunk(part_a, 0, 6, sib_a)
    y_chunk(part_b, first, CHIPS, sib_b)
    y_share(part_a, sib_a, ysend_a, yall_a, 6, OCT)
    y_share(part_b, sib_b, ysend_b, yall_b, CHIPS, 9)
    out_share(yall_a, piece_a, out_a, 0, OCT, 10)
    out_share(yall_b, piece_b, out_b, first, 9, 11)

    def place(pieces, start):
        for tile in range(pieces.shape[2] // LANES):
            rows_f[...] = pieces[:, :, tile * LANES:(tile + 1) * LANES].astype(F32).reshape(LANES, LANES)
            for i in range(OCT):
                lanes = pl.ds(i * dspan + start + tile * LANES, LANES)
                rows = rows_f[pl.ds(i, ROWS, stride=OCT), :]
                out[0, :, lanes] = rows[0:OCT].astype(BF16)
                out[1, :, lanes] = rows[OCT:ROWS].astype(BF16)

    arrived(out_a.at[pl.ds(0, PEERS)], 10)
    place(out_a, 0)
    arrived(out_b.at[pl.ds(0, PEERS)], 11)
    place(out_b, first)
    left(rs1.at[pl.ds(0, CHIPS)], 0)
    left(lat_b.at[pl.ds(0, CHIPS)], 1)
    left(rope_b.at[pl.ds(0, CHIPS)], 2)
    left(lat_b.at[pl.ds(0, OCT)], 12)
    left(rope_b.at[pl.ds(0, OCT)], 13)
    left(q_all.at[pl.ds(0, PEERS)], 3)
    left(o_buf.at[pl.ds(0, PEERS)], 4)
    left(ml_all.at[pl.ds(0, PEERS)], 5)
    left(sib_a, 6)
    left(sib_b, CHIPS)
    left(yall_a.at[pl.ds(0, CHIPS)], OCT)
    left(yall_b.at[pl.ds(0, CHIPS)], 9)
    left(out_a.at[pl.ds(0, PEERS)], 10)
    left(out_b.at[pl.ds(0, PEERS)], 11)


def finish(rows, out, sem):
    copy = pltpu.make_async_copy(rows, out, sem)
    copy.start()
    copy.wait()


def solution(mesh):
    row_spec = P('batch', None)
    cache_spec = P('batch', ('ctx', 'seq'), None)
    proj_spec = P(None, 'seq', None)
    head_spec = P('seq', None, None)

    def local_step(hidden, lengths, latent_cache, rope_keys, w_uq, w_qr, w_uk, w_uv, w_out):
        scale = (w_uq.shape[2] + w_qr.shape[2]) ** -0.5
        width = hidden.shape[1]
        dspan = width // OCT
        first = dspan // LANES // 2 * LANES + LANES
        second = dspan - first
        vmem, dma = pltpu.VMEM, pltpu.SemaphoreType.DMA
        anywhere = pl.BlockSpec(memory_space=pl.ANY)
        scratch = [
            pltpu.SMEM((ROWS,), jnp.int32),
            vmem((2, OCT, dspan), BF16),
            vmem((OCT, width), BF16),
            vmem((dspan, OCT, LANES), BF16),
            vmem((dspan * OCT, LANES), F32),
            vmem((OCT, HALF, dspan), BF16),
            vmem((OCT, LANES, LATENT), BF16),
            vmem((OCT, LATENT, LANES), BF16),
            vmem((OCT, LANES, width), BF16),
            vmem((ROWS, HALF, LATENT), BF16),
            vmem((ROWS, HALF, HALF), BF16),
            vmem((ROWS, HALVED, LANES), BF16),
            vmem((ROWS, HALF, LATENT), BF16),
            vmem((ROWS, HALVED, LANES), BF16),
            vmem((2, LANES, LANES), F32),
            vmem((OCT, 2, ROWS, LANES), F32),
            vmem((2, OCT, QWIDE), BF16),
            vmem((ROWS, OCT, QWIDE), BF16),
            vmem((LANES, WIDE), F32),
            vmem((LANES, WIDE), BF16),
            vmem((ROWS, OCT, LATENT), F32),
            vmem((ROWS, OCT, LATENT), F32),
            vmem((2, LANES), F32),
            vmem((ROWS, 2, LANES), F32),
            vmem((LANES, LANES), F32),
            vmem((2, OCT, first), F32),
            vmem((2, OCT, second), F32),
            vmem((OCT, first), F32),
            vmem((OCT, second), F32),
            vmem((OCT, first), F32),
            vmem((OCT, second), F32),
            vmem((OCT, OCT, first), F32),
            vmem((OCT, OCT, second), F32),
            vmem((OCT, first), BF16),
            vmem((OCT, second), BF16),
            vmem((ROWS, OCT, first), BF16),
            vmem((ROWS, OCT, second), BF16),
            vmem((LANES, LANES), F32),
            dma((10,)), dma((2,)), dma((14,)), dma((14,)), pltpu.SemaphoreType.REGULAR,
        ]
        out = pl.pallas_call(
            functools.partial(kernel, scale),
            out_shape=vmem((2, OCT, width), BF16),
            in_specs=[anywhere] * 9,
            out_specs=pl.BlockSpec(memory_space=pltpu.VMEM),
            scratch_shapes=scratch,
            compiler_params=pltpu.CompilerParams(collective_id=0, has_side_effects=True,
                                                 vmem_limit_bytes=60 * WIDE * WIDE),
            name='mla_decode',
        )(hidden.reshape(2, OCT, width), lengths, latent_cache, rope_keys, w_uq,
          jnp.transpose(w_qr, (1, 2, 0)), w_uk, w_uv, w_out)
        done = pl.pallas_call(
            finish,
            out_shape=jax.ShapeDtypeStruct((2, OCT, width), BF16),
            in_specs=[pl.BlockSpec(memory_space=pltpu.VMEM)],
            out_specs=pl.BlockSpec(memory_space=pl.ANY),
            scratch_shapes=[dma],
            name='mla_out',
        )(pltpu.with_memory_space_constraint(out, pltpu.VMEM))
        return done.reshape(ROWS, width)

    return jax.shard_map(local_step, mesh=mesh,
                         in_specs=(row_spec, P('batch'), cache_spec, cache_spec, proj_spec, proj_spec, head_spec, head_spec, head_spec),
                         out_specs=row_spec, check_vma=False)
```

time: 42.2 us -> 42.3 us (level)
  no operation moved by 1% of the time
where the time goes in v6:
time: 42.3 us; the launch traced here: 42.2 us
  Pallas kernels  42.2 us (100%)
    pallas_call x1, Pallas kernels, local_step(): pl.pallas_call(functools.partial(kernel, scale), out_shape=vmem((2, OCT,...  41.5 us

profile of v6, /device:TPU:1, one launch (start us, length us, event | category | flops | bytes accessed | tf_op | source)
XLA Modules:
  0.0 42.2 jit_solution(1836949582814806051)
XLA Ops:
  0.0 41.5 %mla_decode.1.rows = bf16[2,8,5120]{2,1,0:T(8,128)(2,1)S(1)} custom-call(bf16[2,8,5120]{2,1,0:T(8,128)(2,1)} %bitcast.4, s32[16]{0:T(128)} %lengths.1, bf16[16,64,512]{2,1,0:T(8,128)(2,1)} %latent.1, bf16[16,64,64]{2,1,0:T(8,128)(2,1)} %rope.1, bf16[5120,64,128]{2,1,0:T(8,128)(2,1)} %wuq.1, bf16[64,64,5120]{2,1,0:T(8,128)(2,1)} %bitcast.3, ...), custom_call_target="tpu_custom_call" | custom-call | tf_op jit(solution)/shard_map/mla_decode/pallas_call | solution.py:392
  41.5 0.7 %mla_out.1 = bf16[2,8,5120]{2,1,0:T(8,128)(2,1)} custom-call(bf16[2,8,5120]{2,1,0:T(8,128)(2,1)S(1)} %mla_decode.1.rows), custom_call_target="tpu_custom_call" | custom-call | tf_op jit(solution)/shard_map/mla_out/pallas_call | solution.py:403
